TPU v7x, 256 devices: a whole 4x4x8 slice. The times are simulated.
256 devices in a mesh: row: 16 (over z, x_lo), col: 16 (over x_hi, y, core).
Axes of the slice: x: 4 (x_hi: 2, x_lo: 2; x = x_hi * 2 + x_lo), y: 4, z: 8, core: 2. Of those that a mesh axis runs over, the one named last changes fastest.
Arguments:
- field: bfloat16 [128, 2048, 2048], P(None, 'row', 'col'), may hold values from -6 to 6
- solid_flags: int32 [128, 256, 128], P(None, 'row', 'col'), may hold values 0 or 1
- deriv_matrix: bfloat16 [2048, 2048], replicated, may hold values from -0.125 to 0.125
Outputs:
- filtered: bfloat16 [128, 2048, 2048], P('col', 'row')
- deriv_z: bfloat16 [128, 2048, 2048], P('col', 'row')
Inputs may be any that keep to these rules, and one draw needn't show every extreme that they name: `solid_flags`: 1 marks a solid block, 0 a fluid one.
All inputs are finite; a program needn't handle non-finite values.
Results may differ from a plain program's by a relative error of at most 0.0058.
Values may be sent and summed in bfloat16 or wider, within the bound.
No kernel may reach another device: no remote copies, remote signals or barrier semaphores. Data moves between devices by JAX's collectives and lax.ppermute only.
A program may use at most 64 MiB of HBM per device.

v0:
```python
import jax
import jax.numpy as jnp
from jax import lax
from jax.sharding import PartitionSpec as P

YBLK = 8
ZBLK = 16


filter_taps = ((-3, 1.0), (-2, -6.0), (-1, 15.0), (0, -20.0), (1, 15.0), (2, -6.0), (3, 1.0))


def with_halo(block, sides, width):
    for axis, dim in sides:
        count = lax.axis_size(axis)
        forward = [(i, i + 1) for i in range(count - 1)]
        forward.append((count - 1, 0))
        backward = [(target, source) for source, target in forward]
        low = lax.ppermute(
            lax.slice_in_dim(block, block.shape[dim] - width, None, axis=dim), axis, forward
        )
        high = lax.ppermute(lax.slice_in_dim(block, 0, width, axis=dim), axis, backward)
        block = jnp.concatenate([low, block, high], axis=dim)
    return block


def grouped_exchange(shard, axis, split_dim, concat_dim, work, item_dim, out_dim):
    items = jax.tree.leaves(shard)[0].shape[item_dim]
    count = 2 if items % 2 == 0 else 1
    done = []
    for k in range(count):
        group = jax.tree.map(
            lambda a: lax.slice_in_dim(
                a, k * (items // count), (k + 1) * (items // count), axis=item_dim
            ),
            shard,
        )
        done.append(
            work(
                lax.all_to_all(
                    group, axis, split_axis=split_dim, concat_axis=concat_dim, tiled=True
                )
            )
        )
    return jax.tree.map(lambda *parts: jnp.concatenate(parts, axis=out_dim), *done)


def smooth_padded(padded, axis, length):
    center = lax.slice_in_dim(padded, 3, 3 + length, axis=axis).astype(jnp.float32)
    total = center
    for offset, tap in filter_taps:
        shifted = lax.slice_in_dim(padded, 3 + offset, 3 + offset + length, axis=axis)
        total = total + tap / 64.0 * shifted.astype(jnp.float32)
    return total


def shards(field, solid_flags, deriv_matrix):
    xcount, ycount, zcount = field.shape
    blocks = solid_flags.astype(jnp.float32)
    nyb = blocks.shape[1]
    nzb = blocks.shape[2]
    solid = jnp.broadcast_to(blocks[:, :, None, :, None], (xcount, nyb, YBLK, nzb, ZBLK)).reshape(
        xcount, ycount, zcount
    )
    masked = (field.astype(jnp.float32) * (1.0 - solid)).astype(jnp.bfloat16)
    ypadded = with_halo(masked, (("row", 1),), 3)
    yfilt = smooth_padded(ypadded, 1, ycount).astype(jnp.bfloat16)

    def prepare(lines):
        full = lines.shape[2]
        padded = jnp.concatenate([lines[:, :, full - 3 :], lines, lines[:, :, :3]], axis=2)
        return smooth_padded(padded, 2, full).astype(jnp.bfloat16)

    def finish(lines):
        ready = prepare(lines)
        flat = ready.reshape(-1, ready.shape[2])
        deriv = jnp.dot(flat, deriv_matrix, preferred_element_type=jnp.float32).astype(jnp.bfloat16)
        return (ready, deriv.reshape(ready.shape))

    filtered, deriv_z = grouped_exchange(yfilt, "col", 0, 2, finish, 1, 1)
    return (filtered, deriv_z)


def solution(mesh):
    in_specs = (P(None, "row", "col"), P(None, "row", "col"), P())
    out_specs = (P("col", "row", None), P("col", "row", None))
    return jax.shard_map(shards, mesh=mesh, in_specs=in_specs, out_specs=out_specs, check_vma=False)
```

profile of v0, /device:TPU:1, one launch (start us, length us, event | category | flops | bytes accessed | tf_op | source)
XLA Modules:
  0.0 135.2 jit_solution(9472462184685314685)
XLA Ops:
  0.6 0.8 convert_subtract_fusion
  1.5 6.9 %copy.19 = bf16[128,128,128]{0,2,1:T(8,128)(2,1)} copy(bf16[128,128,128]{2,1,0:T(8,128)(2,1)} %param.3) | data formatting | bytes 8388608 | tf_op args[0]
  8.4 0.9 broadcast_in_dim.2
  9.3 3.5 %multiply_convert_fusion = bf16[128,128,128]{0,2,1:T(8,128)(2,1)S(1)} fusion(f32[128,128,128]{0,2,1:T(8,128)S(1)} %bitcast.23, bf16[128,128,128]{0,2,1:T(8,128)(2,1)} %copy.19), kind=kLoop, calls=%fused_computation.9 | loop fusion | flops 6291456 | bytes 16777216 | tf_op jit(solution)/shard_map/convert_element_type | solution.py:65
  12.8 2.1 %collective-permute-start = (bf16[128,3,128]{0,2,1:T(8,128)(2,1)S(1)}, bf16[128,3,128]{0,2,1:T(8,128)(2,1)S(1)}, u32[]{:S(2)}, u32[]{:S(2)}) collective-permute-start(bf16[128,3,128]{0,2,1:T(8,128)(2,1)S(1)} %get-tuple-element.4), channel_id=1, source_target_pairs={{0,16},{16,32},{32,48},{48,64},{64,80},{80,96},{96,112},{112,128},... | collective-permute-start | bytes 294920 | tf_op jit(solution)/shard_map/ppermute | solution.py:19
  14.9 5.4 %collective-permute-start.1 = (bf16[128,3,128]{0,2,1:T(8,128)(2,1)S(1)}, bf16[128,3,128]{0,2,1:T(8,128)(2,1)S(1)}, u32[]{:S(2)}, u32[]{:S(2)}) collective-permute-start(bf16[128,3,128]{0,2,1:T(8,128)(2,1)S(1)} %get-tuple-element.5), channel_id=1, source_target_pairs={{16,0},{32,16},{48,32},{64,48},{80,64},{96,80},{112,96},{128,112},... | collective-permute-start | bytes 294920 | tf_op jit(solution)/shard_map/ppermute | solution.py:22
  20.3 2.4 %collective-permute-done = bf16[128,3,128]{0,2,1:T(8,128)(2,1)S(1)} collective-permute-done((bf16[128,3,128]{0,2,1:T(8,128)(2,1)S(1)}, bf16[128,3,128]{0,2,1:T(8,128)(2,1)S(1)}, u32[]{:S(2)}, u32[]{:S(2)}) %collective-permute-start) | collective-permute-done | bytes 98336 | tf_op jit(solution)/shard_map/ppermute | solution.py:19
  22.7 0.0 collective-permute-done.1
  22.7 7.6 %fusion.6 = bf16[128,128,128]{0,2,1:T(8,128)(2,1)S(1)} fusion(bf16[128,128,128]{0,2,1:T(8,128)(2,1)S(1)} %multiply_convert_fusion, bf16[128,3,128]{0,2,1:T(8,128)(2,1)S(1)} %collective-permute-done.1, bf16[128,3,128]{0,2,1:T(8,128)(2,1)S(1)} %collective-permute-done), kind=kLoop, calls=%fused_computation.8 | loop fusion | flops 58720256 | bytes 8585216 | tf_op jit(solution)/shard_map/convert_element_type | solution.py:67
  30.3 1.6 %fusion.33 = (bf16[128,64,128]{0,2,1:T(8,128)(2,1)S(1)}, bf16[128,64,128]{0,2,1:T(8,128)(2,1)}) fusion(bf16[128,128,128]{0,2,1:T(8,128)(2,1)S(1)} %fusion.6), kind=kLoop, calls=%fused_computation.65 | loop fusion | bytes 8388608 | tf_op jit(solution)/shard_map/slice | solution.py:33
  31.9 2.8 %copy.20 = bf16[128,64,128]{2,1,0:T(8,128)(2,1)} copy(bf16[128,64,128]{0,2,1:T(8,128)(2,1)S(1)} %get-tuple-element.2) | data formatting | bytes 4194304 | tf_op jit(solution)/shard_map/slice | solution.py:33
  34.6 7.9 %all-to-all-start = ((bf16[128,64,128]{2,1,0:T(8,128)(2,1)}), bf16[128,64,128]{2,1,0:T(8,128)(2,1)S(1)}, u32[]{:S(2)}, u32[]{:S(2)}) async-start(bf16[128,64,128]{2,1,0:T(8,128)(2,1)} %copy.20), calls=%async_computation | async-start | bytes 4194304 | tf_op jit(solution)/shard_map/all_to_all | solution.py:40
  42.5 4.1 %copy.22 = bf16[128,64,128]{2,1,0:T(8,128)(2,1)} copy(bf16[128,64,128]{0,2,1:T(8,128)(2,1)} %get-tuple-element.3) | data formatting | bytes 4194304 | tf_op jit(solution)/shard_map/slice | solution.py:33
  46.7 24.2 %all-to-all-done = bf16[128,64,128]{2,1,0:T(8,128)(2,1)S(1)} async-done(((bf16[128,64,128]{2,1,0:T(8,128)(2,1)}), bf16[128,64,128]{2,1,0:T(8,128)(2,1)S(1)}, u32[]{:S(2)}, u32[]{:S(2)}) %all-to-all-start) | async-done | bytes 2097184 | tf_op jit(solution)/shard_map/all_to_all | solution.py:40
  70.9 0.0 copy-start
  70.9 6.9 %all-to-all-start.1 = ((bf16[128,64,128]{2,1,0:T(8,128)(2,1)}), bf16[128,64,128]{2,1,0:T(8,128)(2,1)}, u32[]{:S(2)}, u32[]{:S(2)}) async-start(bf16[128,64,128]{2,1,0:T(8,128)(2,1)} %copy.22), calls=%async_computation.1 | async-start | bytes 4194304 | tf_op jit(solution)/shard_map/all_to_all | solution.py:40
  77.8 0.0 copy-done
  77.8 2.2 %copy.29 = bf16[16,8,8,8,128]{4,3,0,2,1:T(8,128)(2,1)S(1)} copy(bf16[16,8,8,8,128]{4,3,2,1,0:T(8,128)(2,1)} %bitcast.28) | data formatting | bytes 4194304 | tf_op jit(solution)/shard_map/all_to_all | solution.py:40
  80.0 0.1 fusion.35
  80.1 26.2 %all-to-all-done.1 = bf16[128,64,128]{2,1,0:T(8,128)(2,1)} async-done(((bf16[128,64,128]{2,1,0:T(8,128)(2,1)}), bf16[128,64,128]{2,1,0:T(8,128)(2,1)}, u32[]{:S(2)}, u32[]{:S(2)}) %all-to-all-start.1) | async-done | bytes 2097184 | tf_op jit(solution)/shard_map/all_to_all | solution.py:40
  106.3 0.0 slice-start
  106.3 2.3 %copy.28 = bf16[16,8,8,8,128]{4,3,0,2,1:T(8,128)(2,1)S(1)} copy(bf16[16,8,8,8,128]{4,3,2,1,0:T(8,128)(2,1)} %bitcast.13) | data formatting | bytes 4194304 | tf_op jit(solution)/shard_map/all_to_all | solution.py:40
  108.6 0.1 fusion.36
  108.7 0.0 slice-start.1
  108.7 11.9 %fusion.13 = (bf16[8,64,2048]{2,1,0:T(8,128)(2,1)S(1)}, bf16[8,64,2048]{2,1,0:T(8,128)(2,1)S(1)}) fusion(bf16[8,64,2048]{2,1,0:T(8,128)(2,1)S(1)} %bitcast.25, bf16[8,64,3]{2,1,0:T(8,128)(2,1)S(1)} %get-tuple-element.7, bf16[8,64,3]{2,1,0:T(8,128)(2,1)S(1)} %get-tuple-element.6, bf16[8,64,3]{2,1,0:T(8,128)(2,1)S(1)} %get-tuple-element.9, ...), kind=kLoop, calls=%fused_computation.24 | loop fusion | flops 83886080 | bytes 8400896 | tf_op jit(solution)/shard_map/convert_element_type | solution.py:72
  120.6 2.6 %pad_maximum_fusion.2 = bf16[8,128,2048]{2,1,0:T(8,128)(2,1)} fusion(bf16[8,64,2048]{2,1,0:T(8,128)(2,1)S(1)} %get-tuple-element.11, bf16[8,64,2048]{2,1,0:T(8,128)(2,1)S(1)} %get-tuple-element.10), kind=kLoop, calls=%fused_computation.38 | loop fusion | flops 8388608 | bytes 8388608 | tf_op jit(solution)/shard_map/concatenate | solution.py:45
  123.2 0.0 slice-done
  123.2 0.0 slice-done.1
  123.2 4.7 %convolution_convert_fusion.1 = bf16[512,2048]{1,0:T(8,128)(2,1)S(1)} fusion(bf16[512,2048]{1,0:T(8,128)(2,1)S(1)} %bitcast.30, bf16[2048,2048]{1,0:T(8,128)(2,1)S(1)} %bitcast.34), kind=kOutput, calls=%fused_computation.49 | convolution fusion | flops 4296015872 | bytes 12582912 | tf_op jit(solution)/shard_map/dot_general | solution.py:77
  127.9 4.7 %convolution_convert_fusion = bf16[512,2048]{1,0:T(8,128)(2,1)S(1)} fusion(bf16[512,2048]{1,0:T(8,128)(2,1)S(1)} %bitcast.29, bf16[2048,2048]{1,0:T(8,128)(2,1)S(1)} %bitcast.34), kind=kOutput, calls=%fused_computation.48 | convolution fusion | flops 4296015872 | bytes 12582912 | tf_op jit(solution)/shard_map/dot_general | solution.py:77
  132.6 2.6 %pad_maximum_fusion.3 = bf16[8,128,2048]{2,1,0:T(8,128)(2,1)} fusion(bf16[8,64,2048]{2,1,0:T(8,128)(2,1)S(1)} %bitcast.32, bf16[8,64,2048]{2,1,0:T(8,128)(2,1)S(1)} %bitcast.31), kind=kLoop, calls=%fused_computation.39 | loop fusion | flops 8388608 | bytes 8388608 | tf_op jit(solution)/shard_map/concatenate | solution.py:45
  (2 shorter events, 0.0 us)
Async XLA Ops:
  12.8 9.9 %collective-permute-start = (bf16[128,3,128]{0,2,1:T(8,128)(2,1)S(1)}, bf16[128,3,128]{0,2,1:T(8,128)(2,1)S(1)}, u32[]{:S(2)}, u32[]{:S(2)}) collective-permute-start(bf16[128,3,128]{0,2,1:T(8,128)(2,1)S(1)} %get-tuple-element.4), channel_id=1, source_target_pairs={{0,16},{16,32},{32,48},{48,64},{64,80},{80,96},{96,112},{112,128},... | collective-permute-start | bytes 294920 | tf_op jit(solution)/shard_map/ppermute | solution.py:19
  14.9 7.8 %collective-permute-start.1 = (bf16[128,3,128]{0,2,1:T(8,128)(2,1)S(1)}, bf16[128,3,128]{0,2,1:T(8,128)(2,1)S(1)}, u32[]{:S(2)}, u32[]{:S(2)}) collective-permute-start(bf16[128,3,128]{0,2,1:T(8,128)(2,1)S(1)} %get-tuple-element.5), channel_id=1, source_target_pairs={{16,0},{32,16},{48,32},{64,48},{80,64},{96,80},{112,96},{128,112},... | collective-permute-start | bytes 294920 | tf_op jit(solution)/shard_map/ppermute | solution.py:22
  34.6 36.2 %all-to-all-start = ((bf16[128,64,128]{2,1,0:T(8,128)(2,1)}), bf16[128,64,128]{2,1,0:T(8,128)(2,1)S(1)}, u32[]{:S(2)}, u32[]{:S(2)}) async-start(bf16[128,64,128]{2,1,0:T(8,128)(2,1)} %copy.20), calls=%async_computation | async-start | bytes 4194304 | tf_op jit(solution)/shard_map/all_to_all | solution.py:40
  70.9 6.9 %copy-start = (bf16[128,64,128]{2,1,0:T(8,128)(2,1)}, bf16[128,64,128]{2,1,0:T(8,128)(2,1)S(1)}, u32[]{:S(2)}) copy-start(bf16[128,64,128]{2,1,0:T(8,128)(2,1)S(1)} %all-to-all-done) | copy-start | bytes 6291460
  70.9 35.4 %all-to-all-start.1 = ((bf16[128,64,128]{2,1,0:T(8,128)(2,1)}), bf16[128,64,128]{2,1,0:T(8,128)(2,1)}, u32[]{:S(2)}, u32[]{:S(2)}) async-start(bf16[128,64,128]{2,1,0:T(8,128)(2,1)} %copy.22), calls=%async_computation.1 | async-start | bytes 4194304 | tf_op jit(solution)/shard_map/all_to_all | solution.py:40
  106.3 16.9 %slice-start = ((s8[8388608]{0:T(1024)(128)(4,1)}), s8[4194304]{0:T(1024)(128)(4,1)S(1)}, s32[]{:S(2)}) async-start(s8[8388608]{0:T(1024)(128)(4,1)} %bitcast.33), calls=%async_computation.2 | async-start | bytes 8388608
  108.7 14.5 %slice-start.1 = ((s8[8388608]{0:T(1024)(128)(4,1)}), s8[4194304]{0:T(1024)(128)(4,1)S(1)}, s32[]{:S(2)}) async-start(s8[8388608]{0:T(1024)(128)(4,1)} %bitcast.33), calls=%async_computation.3 | async-start | bytes 8388608
where the time goes:
time: 137 us; the launch traced here: 135 us
  waiting for transfers between devices  52.8 us (39%)
  other arithmetic  29 us (21%)
  starting transfers between devices  22.3 us (16%)
  local copies, waits for them, and re-layouts  21 us (15%)
  matrix products  9.39 us (7%)
    all_to_all x2, waiting for transfers between devices, grouped_exchange(): lax.all_to_all(group, axis, split_axis=split_dim, concat_axis=concat_dim,...  50.4 us
    all_to_all x2, starting transfers between devices, grouped_exchange(): lax.all_to_all(group, axis, split_axis=split_dim, concat_axis=concat_dim,...  14.8 us
    convert_element_type x1, other arithmetic, prepare(): return smooth_padded(padded, 2, full).astype(jnp.bfloat16)  11.9 us
    dot_general x2, matrix products, finish(): jnp.dot(flat, deriv_matrix, preferred_element_type=jnp.float32)  9.39 us
    slice x3, local copies, waits for them, and re-layouts, grouped_exchange(): lax.slice_in_dim(a, k * (items // count), (k + 1) * (items // count), axi...  8.5 us
    convert_element_type x1, other arithmetic, shards(): yfilt = smooth_padded(ypadded, 1, ycount).astype(jnp.bfloat16)  7.55 us
    unnamed x7, local copies, waits for them, and re-layouts  6.91 us
    ppermute x1, starting transfers between devices, with_halo(): lax.ppermute(lax.slice_in_dim(block, 0, width, axis=dim), axis, backward)  5.38 us
  transfers between devices with their start and end apart: 4, of which 3 were waited for; matrix products, arithmetic and copies ran while one was open for 5% of the time, Pallas kernels for 0%

commit v1 on v0

v1 whole, which is shorter than its diff:
```python
import jax
import jax.numpy as jnp
import numpy as np
from jax import lax
from jax.experimental import pallas as pl
from jax.experimental.pallas import tpu as pltpu
from jax.sharding import PartitionSpec as P

YBLK = 8
ZBLK = 16
TAPS = {-3: 1.0, -2: -6.0, -1: 15.0, 0: 44.0, 1: 15.0, 2: -6.0, 3: 1.0}

EDGE = 16
HALO = 4
GROUP = 8


def tap_matrix(out_pos, in_pos):
    mat = np.zeros((len(out_pos), len(in_pos)), np.float32)
    for a, p in enumerate(out_pos):
        for b, q in enumerate(in_pos):
            if q is not None:
                mat[a, b] = TAPS.get(q - p, 0.0) / 64.0
    return mat


def keep_rows(flags_ref, keep_ref, planes):
    nyb, nzb = flags_ref.shape[1:]
    lane = lax.broadcasted_iota(jnp.int32, (nzb, nzb * ZBLK), 1) // ZBLK
    row = lax.broadcasted_iota(jnp.int32, (nzb, nzb * ZBLK), 0)
    spread = (lane == row).astype(jnp.float32)
    keep = (1 - flags_ref[...]).astype(jnp.float32).reshape(planes * nyb, nzb)
    wide = jnp.dot(keep, spread, preferred_element_type=jnp.float32)
    keep_ref[...] = wide.reshape(planes, nyb, nzb * ZBLK)


def masked_rows(field_ref, keep_ref, x, lo, hi):
    parts = []
    for b in range(lo // YBLK, hi // YBLK):
        parts.append(jnp.broadcast_to(keep_ref[x, pl.ds(b, 1), :], (YBLK, keep_ref.shape[2])))
    keep = jnp.concatenate(parts, axis=0)
    return field_ref[x, pl.ds(lo, hi - lo), :].astype(jnp.float32) * keep


def inner_body(field_ref, flags_ref, taps_ref, out_ref, low_ref, high_ref, keep_ref):
    planes, ycount, zcount = field_ref.shape
    keep_rows(flags_ref, keep_ref, planes)
    taps = taps_ref[...]
    for x in range(0, planes, 2):
        pair = []
        for k in range(2):
            m = masked_rows(field_ref, keep_ref, x + k, 0, ycount)
            high_ref[x + k] = m[:HALO].astype(jnp.bfloat16)
            low_ref[x + k] = m[ycount - HALO :].astype(jnp.bfloat16)
            pair.append(m.astype(jnp.bfloat16))
        res = jnp.dot(taps, jnp.concatenate(pair, axis=1), preferred_element_type=jnp.float32)
        for k in range(2):
            out_ref[x + k] = res[:, k * zcount : (k + 1) * zcount].astype(jnp.bfloat16)


def edge_body(field_ref, flags_ref, taps_ref, low_ref, high_ref, out_ref, keep_ref):
    planes, ycount, zcount = field_ref.shape
    keep_rows(flags_ref, keep_ref, planes)
    taps = taps_ref[...]
    for x in range(0, planes, 2):
        pair = []
        for k in range(2):
            top = masked_rows(field_ref, keep_ref, x + k, 0, 2 * EDGE)
            bottom = masked_rows(field_ref, keep_ref, x + k, ycount - 2 * EDGE, ycount)
            halo = jnp.concatenate(
                [low_ref[x + k].astype(jnp.float32), high_ref[x + k].astype(jnp.float32)], axis=0
            )
            halo = jnp.concatenate([halo, jnp.zeros_like(halo)], axis=0)
            pair.append(jnp.concatenate([top, bottom, halo], axis=0).astype(jnp.bfloat16))
        res = jnp.dot(taps, jnp.concatenate(pair, axis=1), preferred_element_type=jnp.float32)
        for k in range(2):
            out_ref[x + k] = res[:, k * zcount : (k + 1) * zcount].astype(jnp.bfloat16)


def inner_filter(field, flags):
    xcount, ycount, zcount = field.shape
    rows = ycount - 2 * EDGE
    taps = jnp.asarray(tap_matrix(range(EDGE, ycount - EDGE), range(ycount)), jnp.bfloat16)
    return pl.pallas_call(
        inner_body,
        grid=(xcount // GROUP,),
        in_specs=[
            pl.BlockSpec((GROUP, ycount, zcount), lambda i: (i, 0, 0)),
            pl.BlockSpec((GROUP,) + flags.shape[1:], lambda i: (i, 0, 0)),
            pl.BlockSpec(taps.shape, lambda i: (0, 0)),
        ],
        out_specs=[
            pl.BlockSpec((GROUP, rows, zcount), lambda i: (i, 0, 0)),
            pl.BlockSpec((GROUP, HALO, zcount), lambda i: (i, 0, 0)),
            pl.BlockSpec((GROUP, HALO, zcount), lambda i: (i, 0, 0)),
        ],
        out_shape=[
            jax.ShapeDtypeStruct((xcount, rows, zcount), jnp.bfloat16),
            jax.ShapeDtypeStruct((xcount, HALO, zcount), jnp.bfloat16),
            jax.ShapeDtypeStruct((xcount, HALO, zcount), jnp.bfloat16),
        ],
        scratch_shapes=[pltpu.VMEM((GROUP, ycount // YBLK, zcount), jnp.float32)],
        compiler_params=pltpu.CompilerParams(vmem_limit_bytes=8 << 20),
        name="inner_filter",
    )(field, flags, taps)


def edge_filter(field, flags, low, high):
    xcount, ycount, zcount = field.shape
    rows = 2 * EDGE
    top = list(range(2 * EDGE))
    bottom = list(range(ycount - 2 * EDGE, ycount))
    halo = list(range(-HALO, 0)) + list(range(ycount, ycount + HALO)) + [None] * (2 * HALO)
    outs = list(range(EDGE)) + list(range(ycount - EDGE, ycount))
    taps = jnp.asarray(tap_matrix(outs, top + bottom + halo), jnp.bfloat16)
    return pl.pallas_call(
        edge_body,
        grid=(xcount // GROUP,),
        in_specs=[
            pl.BlockSpec((GROUP, ycount, zcount), lambda i: (i, 0, 0)),
            pl.BlockSpec((GROUP,) + flags.shape[1:], lambda i: (i, 0, 0)),
            pl.BlockSpec(taps.shape, lambda i: (0, 0)),
            pl.BlockSpec((GROUP, HALO, zcount), lambda i: (i, 0, 0)),
            pl.BlockSpec((GROUP, HALO, zcount), lambda i: (i, 0, 0)),
        ],
        out_specs=pl.BlockSpec((GROUP, rows, zcount), lambda i: (i, 0, 0)),
        out_shape=jax.ShapeDtypeStruct((xcount, rows, zcount), jnp.bfloat16),
        scratch_shapes=[pltpu.VMEM((GROUP, ycount // YBLK, zcount), jnp.float32)],
        compiler_params=pltpu.CompilerParams(vmem_limit_bytes=8 << 20),
        name="edge_filter",
    )(field, flags, taps, low, high)


NBLK = 256


def finish_body(segments, first, *refs):
    slabs_ref, band_ref, deriv_ref = refs[:3]
    filt_out, deriv_out, filt, acc, fsem, dsem = refs[3 if first else 5 :]
    n = pl.program_id(0)
    steps = pl.num_programs(0)
    nslab, planes, rows, zb = slabs_ref.shape

    def filt_copies():
        return [
            pltpu.make_async_copy(
                filt.at[:, pl.ds(src, size), :], filt_out.at[:, pl.ds(dst, size), :], fsem.at[k]
            )
            for k, (src, dst, size) in enumerate(segments)
        ]

    def deriv_copies(step, slot):
        col = pl.multiple_of(step * NBLK, NBLK)
        return [
            pltpu.make_async_copy(
                acc.at[slot, :, pl.ds(src, size), :],
                deriv_out.at[:, pl.ds(dst, size), pl.ds(col, NBLK)],
                dsem.at[slot, k],
            )
            for k, (src, dst, size) in enumerate(segments)
        ]

    @pl.when(n == 0)
    def _():
        band = band_ref[...]
        for j in range(0, nslab, 2):
            window = [
                slabs_ref[(j + d) % nslab].reshape(planes * rows, zb) for d in (-1, 0, 1, 2)
            ]
            res = jnp.dot(
                jnp.concatenate(window, axis=1), band, preferred_element_type=jnp.float32
            )
            filt[:, :, pl.ds(j * zb, 2 * zb)] = res.astype(jnp.bfloat16).reshape(
                planes, rows, 2 * zb
            )
        for copy in filt_copies():
            copy.start()

    slot = n % 2

    @pl.when(n >= 2)
    def _():
        for copy in deriv_copies(n - 2, slot):
            copy.wait()

    flat = filt[...].reshape(planes * rows, nslab * zb)
    res = jnp.dot(flat, deriv_ref[...], preferred_element_type=jnp.float32)
    acc[slot] = res.astype(jnp.bfloat16).reshape(planes, rows, NBLK)
    for copy in deriv_copies(n, slot):
        copy.start()

    @pl.when(n == steps - 1)
    def _():
        for copy in filt_copies():
            copy.wait()
        for copy in deriv_copies(n - 1, 1 - slot):
            copy.wait()
        for copy in deriv_copies(n, slot):
            copy.wait()


def finish(slabs, deriv_matrix, segments, out_shape, partial=None):
    nslab, planes, rows, zb = slabs.shape
    zfull = nslab * zb
    band = jnp.asarray(tap_matrix(range(zb, 3 * zb), range(4 * zb)).T, jnp.bfloat16)
    nseg = len(segments)
    hbm = pl.BlockSpec(memory_space=pl.ANY)
    extra = () if partial is None else partial

    def body(*refs):
        finish_body(segments, partial is None, *refs)

    return pl.pallas_call(
        body,
        grid=(zfull // NBLK,),
        in_specs=[
            pl.BlockSpec(slabs.shape, lambda n: (0, 0, 0, 0)),
            pl.BlockSpec(band.shape, lambda n: (0, 0)),
            pl.BlockSpec((zfull, NBLK), lambda n: (0, n)),
        ]
        + [hbm] * len(extra),
        out_specs=[hbm, hbm],
        out_shape=[jax.ShapeDtypeStruct(out_shape, jnp.bfloat16)] * 2,
        input_output_aliases={} if partial is None else {3: 0, 4: 1},
        scratch_shapes=[
            pltpu.VMEM((planes, rows, zfull), jnp.bfloat16),
            pltpu.VMEM((2, planes, rows, NBLK), jnp.bfloat16),
            pltpu.SemaphoreType.DMA((nseg,)),
            pltpu.SemaphoreType.DMA((2, nseg)),
        ],
        compiler_params=pltpu.CompilerParams(
            dimension_semantics=("arbitrary",), vmem_limit_bytes=32 << 20
        ),
        name="finish_first" if partial is None else "finish_rest",
    )(slabs, band, deriv_matrix, *extra)


def shards(field, solid_flags, deriv_matrix):
    xcount, ycount, zcount = field.shape
    cols = lax.axis_size("col")
    count = lax.axis_size("row")
    inner, low, high = inner_filter(field, solid_flags)
    forward = [(i, (i + 1) % count) for i in range(count)]
    backward = [(target, source) for source, target in forward]
    from_low = lax.ppermute(low, "row", forward)
    from_high = lax.ppermute(high, "row", backward)
    inner_lines = lax.all_to_all(inner, "col", split_axis=0, concat_axis=0, tiled=True)
    edge = edge_filter(field, solid_flags, from_low, from_high)
    edge_lines = lax.all_to_all(edge, "col", split_axis=0, concat_axis=0, tiled=True)
    planes = xcount // cols
    out_shape = (planes, ycount, zcount * cols)
    part = finish(
        inner_lines.reshape(cols, planes, ycount - 2 * EDGE, zcount),
        deriv_matrix,
        ((0, EDGE, ycount - 2 * EDGE),),
        out_shape,
    )
    return tuple(
        finish(
            edge_lines.reshape(cols, planes, 2 * EDGE, zcount),
            deriv_matrix,
            ((0, 0, EDGE), (EDGE, ycount - EDGE, EDGE)),
            out_shape,
            part,
        )
    )


def solution(mesh):
    in_specs = (P(None, "row", "col"), P(None, "row", "col"), P())
    out_specs = (P("col", "row", None), P("col", "row", None))
    return jax.shard_map(shards, mesh=mesh, in_specs=in_specs, out_specs=out_specs, check_vma=False)
```

time: 137 us -> 112 us (0.82)
  Pallas kernels: 0 us -> 29.3 us
  other arithmetic: 29 us -> 0 us
  waiting for transfers between devices: 52.8 us -> 41.2 us
  matrix products: 9.39 us -> 0 us
  local copies, waits for them, and re-layouts: 21 us -> 17.1 us
    all_to_all x2, waiting for transfers between devices: 50.4 us -> 2.02 us  [the longest x1 2.02 us: shards(): lax.all_to_all(edge, 'col', split_axis=0, concat_axis=0, tiled=True)]
    ppermute x2, waiting for transfers between devices: 2.41 us -> 39.2 us  [the longest x1 39.2 us: shards(): from_low = lax.ppermute(low, 'row', forward)]
    pallas_call x0 -> x4, Pallas kernels: none -> 29.3 us  [the longest x2 19.2 us: finish(): pl.pallas_call(body, grid=(zfull // NBLK,), in_specs=[pl.BlockSpec(slabs....]
    convert_element_type x3 -> x0, other arithmetic: 22.9 us -> none  [the longest x1 11.9 us: prepare(): return smooth_padded(padded, 2, full).astype(jnp.bfloat16)]
    unnamed x7 -> x23, local copies, waits for them, and re-layouts: 6.91 us -> 17.1 us
    dot_general x2 -> x0, matrix products: 9.39 us -> none  [finish(): jnp.dot(flat, deriv_matrix, preferred_element_type=jnp.float32)]
    slice x6 -> x0, local copies, waits for them, and re-layouts: 8.74 us -> none  [the longest x3 8.5 us: grouped_exchange(): lax.slice_in_dim(a, k * (items // count), (k + 1) * (items // count), axi...]
    concatenate x2 -> x0, other arithmetic: 5.2 us -> none  [grouped_exchange(): jnp.concatenate(parts, axis=out_dim)]
  transfers between devices with their start and end apart: 4 -> 4, of which waited for: 3 -> 2; matrix products, arithmetic and copies ran while one was open for 5% -> 0% of each run, Pallas kernels for 0% -> 15%
where the time goes in v1:
time: 112 us; the launch traced here: 111 us
  waiting for transfers between devices  41.2 us (37%)
  Pallas kernels  29.3 us (26%)
  starting transfers between devices  22.9 us (20%)
  local copies, waits for them, and re-layouts  17.1 us (15%)
    ppermute x1, waiting for transfers between devices, shards(): from_low = lax.ppermute(low, 'row', forward)  39.2 us
    pallas_call x2, Pallas kernels, finish(): pl.pallas_call(body, grid=(zfull // NBLK,), in_specs=[pl.BlockSpec(slabs....  19.2 us
    unnamed x23, local copies, waits for them, and re-layouts  17.1 us
    all_to_all x1, starting transfers between devices, shards(): lax.all_to_all(edge, 'col', split_axis=0, concat_axis=0, tiled=True)  8.64 us
    all_to_all x1, starting transfers between devices, shards(): lax.all_to_all(inner, 'col', split_axis=0, concat_axis=0, tiled=True)  8.56 us
    pallas_call x1, Pallas kernels, inner_filter(): pl.pallas_call(inner_body, grid=(xcount // GROUP,), in_specs=[pl.BlockSpe...  5.52 us
    ppermute x1, starting transfers between devices, shards(): from_high = lax.ppermute(high, 'row', backward)  5.38 us
    pallas_call x1, Pallas kernels, edge_filter(): pl.pallas_call(edge_body, grid=(xcount // GROUP,), in_specs=[pl.BlockSpec...  4.59 us
  transfers between devices with their start and end apart: 4, of which 2 were waited for; matrix products, arithmetic and copies ran while one was open for 0% of the time, Pallas kernels for 15%

profile of v1, /device:TPU:1, one launch (start us, length us, event | category | flops | bytes accessed | tf_op | source)
XLA Modules:
  0.0 111.2 jit_solution(4974417937243270987)
XLA Ops:
  0.6 1.3 %copy.12.flags_ref = s32[128,16,8]{2,1,0:T(8,128)S(1)} copy(s32[128,16,8]{0,2,1:T(8,128)} %param.8) | data formatting | bytes 131072 | tf_op args[1]
  2.0 0.0 copy-start.2
  2.0 2.2 %copy-done.2 = bf16[128,128,128]{2,1,0:T(8,128)(2,1)S(1)} copy-done((bf16[128,128,128]{2,1,0:T(8,128)(2,1)S(1)}, bf16[128,128,128]{2,1,0:T(8,128)(2,1)}, u32[]{:S(2)}) %copy-start.2) | copy-done | bytes 4194328
  4.1 0.0 copy-start.9
  4.1 0.7 copy-done.9
  4.9 0.0 copy-start.4
  4.9 5.5 %inner_filter.1 = (bf16[128,96,128]{2,1,0:T(8,128)(2,1)S(1)}, bf16[128,4,128]{2,1,0:T(4,128)(2,1)S(1)}, bf16[128,4,128]{2,1,0:T(4,128)(2,1)S(1)}) custom-call(bf16[128,128,128]{2,1,0:T(8,128)(2,1)S(1)} %copy-done.2, s32[128,16,8]{2,1,0:T(8,128)S(1)} %copy.12.flags_ref, bf16[96,128]{1,0:T(8,128)(2,1)S(1)} %copy-done.9), custom_call_target="tpu_custom_call" | custom-call | tf_op jit(solution)/shard_map/inner_filter/pallas_call | solution.py:84
  10.4 0.0 copy-start.7
  10.4 1.7 %copy-done.7 = bf16[128,96,128]{2,1,0:T(8,128)(2,1)} copy-done((bf16[128,96,128]{2,1,0:T(8,128)(2,1)}, bf16[128,96,128]{2,1,0:T(8,128)(2,1)S(1)}, u32[]{:S(2)}) %copy-start.7) | copy-done | bytes 3145752
  12.1 0.0 copy-start.10
  12.1 0.0 copy-done.4
  12.1 8.6 %all-to-all-start.1 = ((bf16[128,96,128]{2,1,0:T(8,128)(2,1)}), bf16[128,96,128]{2,1,0:T(8,128)(2,1)S(1)}, u32[]{:S(2)}, u32[]{:S(2)}) async-start(bf16[128,96,128]{2,1,0:T(8,128)(2,1)} %copy-done.7), calls=%async_computation.1 | async-start | bytes 6291456 | tf_op jit(solution)/shard_map/all_to_all | solution.py:247
  20.6 0.3 collective-permute-start
  21.0 5.4 %collective-permute-start.1 = (bf16[128,4,128]{2,1,0:T(4,128)(2,1)S(1)}, bf16[128,4,128]{2,1,0:T(4,128)(2,1)S(1)}, u32[]{:S(2)}, u32[]{:S(2)}) collective-permute-start(bf16[128,4,128]{2,1,0:T(4,128)(2,1)S(1)} %get-tuple-element.8), channel_id=1, source_target_pairs={{16,0},{32,16},{48,32},{64,48},{80,64},{96,80},{112,96},{128,112},... | collective-permute-start | bytes 393224 | tf_op jit(solution)/shard_map/ppermute | solution.py:246
  26.3 39.2 %collective-permute-done.low_ref = bf16[128,4,128]{2,1,0:T(4,128)(2,1)S(1)} collective-permute-done((bf16[128,4,128]{2,1,0:T(4,128)(2,1)S(1)}, bf16[128,4,128]{2,1,0:T(4,128)(2,1)S(1)}, u32[]{:S(2)}, u32[]{:S(2)}) %collective-permute-start) | collective-permute-done | bytes 131104 | tf_op jit(solution)/shard_map/ppermute | solution.py:245
  65.5 0.0 collective-permute-done.1.high_ref
  65.5 0.0 copy-done.10
  65.5 0.0 copy-start.3
  65.5 2.2 %copy-done.3 = bf16[128,128,128]{2,1,0:T(8,128)(2,1)S(1)} copy-done((bf16[128,128,128]{2,1,0:T(8,128)(2,1)S(1)}, bf16[128,128,128]{2,1,0:T(8,128)(2,1)}, u32[]{:S(2)}) %copy-start.3) | copy-done | bytes 4194328
  67.7 0.0 copy-start.5
  67.7 1.2 %copy-done.5 = s32[128,16,8]{2,1,0:T(8,128)S(1)} copy-done((s32[128,16,8]{2,1,0:T(8,128)S(1)}, s32[128,16,8]{2,1,0:T(8,128)}, u32[]{:S(2)}) %copy-start.5) | copy-done | bytes 65560
  69.0 0.0 copy-start.8
  69.0 4.6 %edge_filter.1 = bf16[128,32,128]{2,1,0:T(8,128)(2,1)S(1)} custom-call(bf16[128,128,128]{2,1,0:T(8,128)(2,1)S(1)} %copy-done.3, s32[128,16,8]{2,1,0:T(8,128)S(1)} %copy-done.5, bf16[32,80]{1,0:T(8,128)(2,1)S(1)} %copy-done.10, bf16[128,4,128]{2,1,0:T(4,128)(2,1)S(1)} %collective-permute-done.low_ref, bf16[128,4,128]{2,1,0:T(4,128)(2,1)S(1)} %collective-permute-done.1.high_ref), custom_call_target="tpu_custom_call" | custom-call | tf_op jit(solution)/shard_map/edge_filter/pallas_call | solution.py:116
  73.6 0.0 copy-start.6
  73.6 1.0 copy-done.6
  74.6 0.0 all-to-all-done.1
  74.6 8.6 %all-to-all-start = ((bf16[128,32,128]{2,1,0:T(8,128)(2,1)}), bf16[128,32,128]{2,1,0:T(8,128)(2,1)}, u32[]{:S(2)}, u32[]{:S(2)}) async-start(bf16[128,32,128]{2,1,0:T(8,128)(2,1)} %copy-done.6), calls=%async_computation | async-start | bytes 2097152 | tf_op jit(solution)/shard_map/all_to_all | solution.py:249
  83.2 0.0 copy-done.8
  83.2 0.0 copy-start
  83.2 3.4 %copy-done = bf16[2048,2048]{1,0:T(8,128)(2,1)S(1)} copy-done((bf16[2048,2048]{1,0:T(8,128)(2,1)S(1)}, bf16[2048,2048]{1,0:T(8,128)(2,1)}, u32[]{:S(2)}) %copy-start) | copy-done | bytes 8388632
  86.6 11.8 %finish_first.1 = (bf16[8,128,2048]{2,1,0:T(8,128)(2,1)}, bf16[8,128,2048]{2,1,0:T(8,128)(2,1)}) custom-call(bf16[16,8,96,128]{3,2,1,0:T(8,128)(2,1)S(1)} %bitcast.2, bf16[512,256]{1,0:T(8,128)(2,1)S(1)} %copy-done.8, bf16[2048,2048]{1,0:T(8,128)(2,1)S(1)} %copy-done), custom_call_target="tpu_custom_call" | custom-call | tf_op jit(solution)/shard_map/finish_first/pallas_call | solution.py:213
  98.4 2.0 %all-to-all-done = bf16[128,32,128]{2,1,0:T(8,128)(2,1)} async-done(((bf16[128,32,128]{2,1,0:T(8,128)(2,1)}), bf16[128,32,128]{2,1,0:T(8,128)(2,1)}, u32[]{:S(2)}, u32[]{:S(2)}) %all-to-all-start) | async-done | bytes 1048608 | tf_op jit(solution)/shard_map/all_to_all | solution.py:249
  100.4 0.0 copy-start.1
  100.4 3.4 %copy-done.1 = bf16[2048,2048]{1,0:T(8,128)(2,1)S(1)} copy-done((bf16[2048,2048]{1,0:T(8,128)(2,1)S(1)}, bf16[2048,2048]{1,0:T(8,128)(2,1)}, u32[]{:S(2)}) %copy-start.1) | copy-done | bytes 8388632
  103.8 7.4 %finish_rest.1 = (bf16[8,128,2048]{2,1,0:T(8,128)(2,1)}, bf16[8,128,2048]{2,1,0:T(8,128)(2,1)}) custom-call(bf16[16,8,32,128]{3,2,1,0:T(8,128)(2,1)} %bitcast.refs_0_, bf16[512,256]{1,0:T(8,128)(2,1)S(1)} %copy-done.8, bf16[2048,2048]{1,0:T(8,128)(2,1)S(1)} %copy-done.1, ...), custom_call_target="tpu_custom_call", output_to_operand_aliasing={{0}: (3, {}), {1}: (4, {})} | custom-call | tf_op jit(solution)/shard_map/finish_rest/pallas_call | solution.py:213
Async XLA Ops:
  2.0 2.2 %copy-start.2 = (bf16[128,128,128]{2,1,0:T(8,128)(2,1)S(1)}, bf16[128,128,128]{2,1,0:T(8,128)(2,1)}, u32[]{:S(2)}) copy-start(bf16[128,128,128]{2,1,0:T(8,128)(2,1)} %field_ref.3) | copy-start | bytes 12582916
  4.1 0.7 copy-start.9
  4.9 7.2 %copy-start.4 = (s32[128,16,8]{2,1,0:T(8,128)}, s32[128,16,8]{2,1,0:T(8,128)S(1)}, u32[]{:S(2)}) copy-start(s32[128,16,8]{2,1,0:T(8,128)S(1)} %copy.12.flags_ref) | copy-start | bytes 196612
  10.4 1.7 %copy-start.7 = (bf16[128,96,128]{2,1,0:T(8,128)(2,1)}, bf16[128,96,128]{2,1,0:T(8,128)(2,1)S(1)}, u32[]{:S(2)}) copy-start(bf16[128,96,128]{2,1,0:T(8,128)(2,1)S(1)} %get-tuple-element.9) | copy-start | bytes 9437188
  12.1 53.5 %copy-start.10 = (bf16[32,80]{1,0:T(8,128)(2,1)S(1)}, bf16[32,80]{1,0:T(8,128)(2,1)}, u32[]{:S(2)}) copy-start(bf16[32,80]{1,0:T(8,128)(2,1)} %constant.7.clone.taps_ref) | copy-start | bytes 15364
  12.1 62.5 %all-to-all-start.1 = ((bf16[128,96,128]{2,1,0:T(8,128)(2,1)}), bf16[128,96,128]{2,1,0:T(8,128)(2,1)S(1)}, u32[]{:S(2)}, u32[]{:S(2)}) async-start(bf16[128,96,128]{2,1,0:T(8,128)(2,1)} %copy-done.7), calls=%async_computation.1 | async-start | bytes 6291456 | tf_op jit(solution)/shard_map/all_to_all | solution.py:247
  20.6 44.9 %collective-permute-start = (bf16[128,4,128]{2,1,0:T(4,128)(2,1)S(1)}, bf16[128,4,128]{2,1,0:T(4,128)(2,1)S(1)}, u32[]{:S(2)}, u32[]{:S(2)}) collective-permute-start(bf16[128,4,128]{2,1,0:T(4,128)(2,1)S(1)} %get-tuple-element.7), channel_id=1, source_target_pairs={{0,16},{16,32},{32,48},{48,64},{64,80},{80,96},{96,112},{112,128},... | collective-permute-start | bytes 393224 | tf_op jit(solution)/shard_map/ppermute | solution.py:245
  21.0 44.6 %collective-permute-start.1 = (bf16[128,4,128]{2,1,0:T(4,128)(2,1)S(1)}, bf16[128,4,128]{2,1,0:T(4,128)(2,1)S(1)}, u32[]{:S(2)}, u32[]{:S(2)}) collective-permute-start(bf16[128,4,128]{2,1,0:T(4,128)(2,1)S(1)} %get-tuple-element.8), channel_id=1, source_target_pairs={{16,0},{32,16},{48,32},{64,48},{80,64},{96,80},{112,96},{128,112},... | collective-permute-start | bytes 393224 | tf_op jit(solution)/shard_map/ppermute | solution.py:246
  65.5 2.2 %copy-start.3 = (bf16[128,128,128]{2,1,0:T(8,128)(2,1)S(1)}, bf16[128,128,128]{2,1,0:T(8,128)(2,1)}, u32[]{:S(2)}) copy-start(bf16[128,128,128]{2,1,0:T(8,128)(2,1)} %field_ref.3) | copy-start | bytes 12582916
  67.7 1.2 %copy-start.5 = (s32[128,16,8]{2,1,0:T(8,128)S(1)}, s32[128,16,8]{2,1,0:T(8,128)}, u32[]{:S(2)}) copy-start(s32[128,16,8]{2,1,0:T(8,128)} %copy-done.4) | copy-start | bytes 196612
  69.0 14.2 %copy-start.8 = (bf16[512,256]{1,0:T(8,128)(2,1)S(1)}, bf16[512,256]{1,0:T(8,128)(2,1)}, u32[]{:S(2)}) copy-start(bf16[512,256]{1,0:T(8,128)(2,1)} %constant.8.clone.refs_1_) | copy-start | bytes 786436
  73.6 1.0 copy-start.6
  74.6 25.8 %all-to-all-start = ((bf16[128,32,128]{2,1,0:T(8,128)(2,1)}), bf16[128,32,128]{2,1,0:T(8,128)(2,1)}, u32[]{:S(2)}, u32[]{:S(2)}) async-start(bf16[128,32,128]{2,1,0:T(8,128)(2,1)} %copy-done.6), calls=%async_computation | async-start | bytes 2097152 | tf_op jit(solution)/shard_map/all_to_all | solution.py:249
  83.2 3.4 %copy-start = (bf16[2048,2048]{1,0:T(8,128)(2,1)S(1)}, bf16[2048,2048]{1,0:T(8,128)(2,1)}, u32[]{:S(2)}) copy-start(bf16[2048,2048]{1,0:T(8,128)(2,1)} %refs_2_.3) | copy-start | bytes 25165828
  100.4 3.4 %copy-start.1 = (bf16[2048,2048]{1,0:T(8,128)(2,1)S(1)}, bf16[2048,2048]{1,0:T(8,128)(2,1)}, u32[]{:S(2)}) copy-start(bf16[2048,2048]{1,0:T(8,128)(2,1)} %refs_2_.3) | copy-start | bytes 25165828

commit v2 on v1

v2 whole, which is shorter than its diff:
```python
import jax
import jax.numpy as jnp
import numpy as np
from jax import lax
from jax.experimental import pallas as pl
from jax.experimental.pallas import tpu as pltpu
from jax.sharding import PartitionSpec as P


YBLK = 8
ZBLK = 16
TAPS = {-3: 1.0, -2: -6.0, -1: 15.0, 0: 44.0, 1: 15.0, 2: -6.0, 3: 1.0}

EDGE = 16
HALO = 4
GROUP = 8
FIRST = 4
TILE = 16
ORDER = (
    (1, 0, 0), (0, 1, 0), (1, 1, 0), (0, 3, 0), (1, 3, 0),
    (0, 2, 0), (1, 2, 0), (0, 1, 1), (1, 0, 1), (0, 3, 1),
    (1, 1, 1), (0, 2, 1), (1, 3, 1), (1, 2, 1), (0, 0, 1),
)
OWN = (0, 0, 0)
BIG = 60 << 20


def tap_matrix(out_pos, in_pos):
    mat = np.zeros((len(out_pos), len(in_pos)), np.float32)
    for a, p in enumerate(out_pos):
        for b, q in enumerate(in_pos):
            if q is not None:
                mat[a, b] = TAPS.get(q - p, 0.0) / 64.0
    return mat


def shifted(index, offset, sign):
    x, y, c = index // 8, (index // 2) % 4, index % 2
    dx, dy, dc = offset
    return ((x + dx) % 2) * 8 + ((y + sign * dy + 4) % 4) * 2 + (c + dc) % 2


def expand_flags(flags_ref, keep_ref):
    nyb, nzb, _ = flags_ref.shape
    lane = lax.broadcasted_iota(jnp.int32, (nzb, nzb * ZBLK), 1) // ZBLK
    row = lax.broadcasted_iota(jnp.int32, (nzb, nzb * ZBLK), 0)
    spread = (lane == row).astype(jnp.float32)
    for b in range(nyb):
        keep = (1 - flags_ref[b]).astype(jnp.float32)
        keep_ref[b] = lax.dot_general(
            keep, spread, (((0,), (0,)), ((), ())), preferred_element_type=jnp.float32
        )


def masked_tile(rows, keep_ref, x, t):
    zcount = keep_ref.shape[2]
    keep = jnp.concatenate(
        [
            jnp.broadcast_to(keep_ref[b, pl.ds(x, 1), :], (YBLK, zcount))
            for b in range(t * TILE // YBLK, (t + 1) * TILE // YBLK)
        ],
        axis=0,
    )
    return rows * keep.astype(jnp.bfloat16)


def group_copies(field_ref, fbuf, sem, offsets, me):
    copies = []
    for k, offset in enumerate(offsets):
        start = pl.multiple_of(shifted(me, offset, 1) * GROUP, GROUP)
        copies.append(pltpu.make_async_copy(field_ref.at[pl.ds(start, GROUP)], fbuf.at[k], sem.at[k]))
    return copies


def filter_group(fbuf, k, base, keep_ref, taps, out_ref):
    _, planes, ycount, zcount = fbuf.shape
    for p in range(0, planes, 2):
        pair = []
        for q in (p, p + 1):
            tiles = [
                masked_tile(fbuf[k, q, pl.ds(t * TILE, TILE), :], keep_ref, base + q, t)
                for t in range(ycount // TILE)
            ]
            pair.append(jnp.concatenate(tiles, axis=0))
        res = jnp.dot(taps, jnp.concatenate(pair, axis=1), preferred_element_type=jnp.float32)
        out_ref[p] = res[:, :zcount].astype(jnp.bfloat16)
        out_ref[p + 1] = res[:, zcount:].astype(jnp.bfloat16)


def first_body(field_ref, flags_ref, taps_ref, *refs):
    outs, (keep_ref, fbuf, sem) = refs[:FIRST], refs[FIRST:]
    me = lax.axis_index("col")
    copies = group_copies(field_ref, fbuf, sem, ORDER[:FIRST], me)
    for copy in copies:
        copy.start()
    expand_flags(flags_ref, keep_ref)
    taps = taps_ref[...]
    for k, offset in enumerate(ORDER[:FIRST]):
        copies[k].wait()
        filter_group(fbuf, k, shifted(me, offset, 1) * GROUP, keep_ref, taps, outs[k])


def rest_body(field_ref, keep_ref, taps_ref, *refs):
    offsets = ORDER[FIRST:] + (OWN,) + ORDER[:FIRST]
    nout = len(ORDER) + 1 - FIRST
    outs, (low_ref, high_ref, fbuf, sem) = refs[:nout], refs[nout:]
    ycount, _ = fbuf.shape[2:]
    me = lax.axis_index("col")
    copies = group_copies(field_ref, fbuf, sem, offsets, me)
    for copy in copies:
        copy.start()
    taps = taps_ref[...]
    for k, offset in enumerate(offsets):
        copies[k].wait()
        base = shifted(me, offset, 1) * GROUP
        if k < nout:
            filter_group(fbuf, k, base, keep_ref, taps, outs[k])
        last = ycount // TILE - 1
        for q in range(GROUP):
            top = masked_tile(fbuf[k, q, pl.ds(0, TILE), :], keep_ref, base + q, 0)
            end = masked_tile(fbuf[k, q, pl.ds(last * TILE, TILE), :], keep_ref, base + q, last)
            high_ref[base + q] = top[:HALO]
            low_ref[base + q] = end[TILE - HALO :]


def inner_filter(field, flags):
    xcount, ycount, zcount = field.shape
    rows = ycount - 2 * EDGE
    taps = jnp.asarray(tap_matrix(range(EDGE, ycount - EDGE), range(ycount)), jnp.bfloat16)
    message = jax.ShapeDtypeStruct((GROUP, rows, zcount), jnp.bfloat16)
    halo = jax.ShapeDtypeStruct((xcount, HALO, zcount), jnp.bfloat16)
    keep = jax.ShapeDtypeStruct((ycount // YBLK, xcount, zcount), jnp.float32)
    hbm = pl.BlockSpec(memory_space=pl.ANY)
    vmem = pl.BlockSpec(memory_space=pltpu.VMEM)
    params = pltpu.CompilerParams(vmem_limit_bytes=24 << 20)

    def scratch(count):
        return [
            pltpu.VMEM((count, GROUP, ycount, zcount), jnp.bfloat16),
            pltpu.SemaphoreType.DMA((count,)),
        ]

    *sent, keep = pl.pallas_call(
        first_body,
        in_specs=[hbm, vmem, vmem],
        out_specs=[vmem] * (FIRST + 1),
        out_shape=[message] * FIRST + [keep],
        scratch_shapes=scratch(FIRST),
        compiler_params=params,
        name="first_messages",
    )(field, flags, taps)
    nout = len(ORDER) + 1 - FIRST
    *others, low, high = pl.pallas_call(
        rest_body,
        in_specs=[hbm, vmem, vmem],
        out_specs=[vmem] * (nout + 2),
        out_shape=[message] * nout + [halo, halo],
        scratch_shapes=scratch(len(ORDER) + 1),
        compiler_params=params,
        name="rest_messages",
    )(field, keep, taps)
    return sent + others, low, high, keep


def edge_body(field_ref, keep_ref, taps_ref, low_ref, high_ref, out_ref):
    planes, ycount, zcount = field_ref.shape
    taps = taps_ref[...]
    need = 2 * EDGE
    ntile = ycount // TILE
    picks = list(range(need // TILE)) + list(range(ntile - need // TILE, ntile))
    for x in range(0, planes, 2):
        pair = []
        for k in (x, x + 1):
            tiles = [masked_tile(field_ref[k, pl.ds(t * TILE, TILE), :], keep_ref, k, t) for t in picks]
            halo = jnp.concatenate(
                [low_ref[k].astype(jnp.float32), high_ref[k].astype(jnp.float32)], axis=0
            )
            halo = jnp.concatenate([halo, jnp.zeros_like(halo)], axis=0)
            pair.append(jnp.concatenate(tiles + [halo.astype(jnp.bfloat16)], axis=0))
        res = jnp.dot(taps, jnp.concatenate(pair, axis=1), preferred_element_type=jnp.float32)
        out_ref[x] = res[:, :zcount].astype(jnp.bfloat16)
        out_ref[x + 1] = res[:, zcount:].astype(jnp.bfloat16)


def edge_filter(field, keep, low, high):
    xcount, ycount, zcount = field.shape
    rows = 2 * EDGE
    top = list(range(2 * EDGE))
    bottom = list(range(ycount - 2 * EDGE, ycount))
    halo = list(range(-HALO, 0)) + list(range(ycount, ycount + HALO)) + [None] * (2 * HALO)
    outs = list(range(EDGE)) + list(range(ycount - EDGE, ycount))
    taps = jnp.asarray(tap_matrix(outs, top + bottom + halo), jnp.bfloat16)
    size = 2 * GROUP
    return pl.pallas_call(
        edge_body,
        grid=(xcount // size,),
        in_specs=[
            pl.BlockSpec((size, ycount, zcount), lambda i: (i, 0, 0)),
            pl.BlockSpec((keep.shape[0], size, zcount), lambda i: (0, i, 0)),
            pl.BlockSpec(taps.shape, lambda i: (0, 0)),
            pl.BlockSpec((size, HALO, zcount), lambda i: (i, 0, 0)),
            pl.BlockSpec((size, HALO, zcount), lambda i: (i, 0, 0)),
        ],
        out_specs=pl.BlockSpec((size, rows, zcount), lambda i: (i, 0, 0)),
        out_shape=jax.ShapeDtypeStruct((xcount, rows, zcount), jnp.bfloat16),
        compiler_params=pltpu.CompilerParams(vmem_limit_bytes=16 << 20),
        name="edge_filter",
    )(field, keep, taps, low, high)


NBLK = 256


def finish_body(segments, nin, nskip, *refs):
    lines, (band_ref, deriv_ref) = refs[:nin], refs[nin : nin + 2]
    filt_out, deriv_out, slabs_ref, filt, acc, ssem, fsem, dsem = refs[nin + 2 + nskip :]
    n = pl.program_id(0)
    steps = pl.num_programs(0)
    nslab, planes, rows, zb = slabs_ref.shape

    def slab_copies():
        if nin == 1:
            return [pltpu.make_async_copy(lines[0], slabs_ref, ssem.at[0])]
        me = lax.axis_index("col")
        return [
            pltpu.make_async_copy(line, slabs_ref.at[shifted(me, offset, -1)], ssem.at[k])
            for k, (line, offset) in enumerate(zip(lines, ORDER + (OWN,)))
        ]

    def filt_copies():
        return [
            pltpu.make_async_copy(
                filt.at[:, pl.ds(src, size), :], filt_out.at[:, pl.ds(dst, size), :], fsem.at[k]
            )
            for k, (src, dst, size) in enumerate(segments)
        ]

    def deriv_copies(step, slot):
        col = pl.multiple_of(step * NBLK, NBLK)
        return [
            pltpu.make_async_copy(
                acc.at[slot, :, pl.ds(src, size), :],
                deriv_out.at[:, pl.ds(dst, size), pl.ds(col, NBLK)],
                dsem.at[slot, k],
            )
            for k, (src, dst, size) in enumerate(segments)
        ]

    @pl.when(n == 0)
    def _():
        copies = slab_copies()
        for copy in copies:
            copy.start()
        for copy in copies:
            copy.wait()
        band = band_ref[...]
        for j in range(0, nslab, 2):
            window = [
                slabs_ref[(j + d) % nslab].reshape(planes * rows, zb) for d in (-1, 0, 1, 2)
            ]
            res = jnp.dot(
                jnp.concatenate(window, axis=1), band, preferred_element_type=jnp.float32
            )
            filt[:, :, pl.ds(j * zb, 2 * zb)] = res.astype(jnp.bfloat16).reshape(
                planes, rows, 2 * zb
            )
        for copy in filt_copies():
            copy.start()

    slot = n % 2

    @pl.when(n >= 2)
    def _():
        for copy in deriv_copies(n - 2, slot):
            copy.wait()

    flat = filt[...].reshape(planes * rows, nslab * zb)
    res = jnp.dot(flat, deriv_ref[...], preferred_element_type=jnp.float32)
    acc[slot] = res.astype(jnp.bfloat16).reshape(planes, rows, NBLK)
    for copy in deriv_copies(n, slot):
        copy.start()

    @pl.when(n == steps - 1)
    def _():
        for copy in filt_copies():
            copy.wait()
        for copy in deriv_copies(n - 1, 1 - slot):
            copy.wait()
        for copy in deriv_copies(n, slot):
            copy.wait()


def finish(lines, deriv_matrix, slab_shape, segments, out_shape, partial=()):
    nslab, planes, rows, zb = slab_shape
    zfull = nslab * zb
    band = jnp.asarray(tap_matrix(range(zb, 3 * zb), range(4 * zb)).T, jnp.bfloat16)
    nseg = len(segments)
    nin = len(lines)
    hbm = pl.BlockSpec(memory_space=pl.ANY)

    def body(*refs):
        finish_body(segments, nin, len(partial), *refs)

    return pl.pallas_call(
        body,
        grid=(zfull // NBLK,),
        in_specs=[hbm] * nin
        + [
            pl.BlockSpec(band.shape, lambda n: (0, 0)),
            pl.BlockSpec((zfull, NBLK), lambda n: (0, n)),
        ]
        + [hbm] * len(partial),
        out_specs=[hbm, hbm],
        out_shape=[jax.ShapeDtypeStruct(out_shape, jnp.bfloat16)] * 2,
        input_output_aliases={nin + 2 + k: k for k in range(len(partial))},
        scratch_shapes=[
            pltpu.VMEM(slab_shape, jnp.bfloat16),
            pltpu.VMEM((planes, rows, zfull), jnp.bfloat16),
            pltpu.VMEM((2, planes, rows, NBLK), jnp.bfloat16),
            pltpu.SemaphoreType.DMA((nin,)),
            pltpu.SemaphoreType.DMA((nseg,)),
            pltpu.SemaphoreType.DMA((2, nseg)),
        ],
        compiler_params=pltpu.CompilerParams(
            dimension_semantics=("arbitrary",), vmem_limit_bytes=BIG
        ),
        name="finish_rest" if partial else "finish_first",
    )(*lines, band, deriv_matrix, *partial)


def shards(field, solid_flags, deriv_matrix):
    xcount, ycount, zcount = field.shape
    cols = lax.axis_size("col")
    count = lax.axis_size("row")
    planes = xcount // cols
    out_shape = (planes, ycount, zcount * cols)
    messages, low, high, keep = inner_filter(field, solid_flags.transpose(1, 2, 0))
    lines = []
    for k, offset in enumerate(ORDER):
        pairs = [(i, shifted(i, offset, 1)) for i in range(cols)]
        lines.append(lax.ppermute(messages[k], "col", pairs))
    lines.append(messages[-1])
    forward = [(i, (i + 1) % count) for i in range(count)]
    backward = [(target, source) for source, target in forward]
    from_low = lax.ppermute(low, "row", forward)
    from_high = lax.ppermute(high, "row", backward)
    edge = edge_filter(field, keep, from_low, from_high)
    edge_lines = lax.all_to_all(edge, "col", split_axis=0, concat_axis=0, tiled=True)
    part = finish(
        lines,
        deriv_matrix,
        (cols, planes, ycount - 2 * EDGE, zcount),
        ((0, EDGE, ycount - 2 * EDGE),),
        out_shape,
    )
    slab_shape = (cols, planes, 2 * EDGE, zcount)
    return tuple(
        finish(
            [edge_lines.reshape(slab_shape)],
            deriv_matrix,
            slab_shape,
            ((0, 0, EDGE), (EDGE, ycount - EDGE, EDGE)),
            out_shape,
            tuple(part),
        )
    )


def solution(mesh):
    in_specs = (P(None, "row", "col"), P(None, "row", "col"), P())
    out_specs = (P("col", "row", None), P("col", "row", None))
    return jax.shard_map(shards, mesh=mesh, in_specs=in_specs, out_specs=out_specs, check_vma=False)
```

time: 112 us -> 114 us (1.018)
  starting transfers between devices: 22.9 us -> 46.7 us
  waiting for transfers between devices: 41.2 us -> 27 us
  local copies, waits for them, and re-layouts: 17.1 us -> 5.13 us
  Pallas kernels: 29.3 us -> 33.9 us
    ppermute x1, waiting for transfers between devices: 39.2 us -> 3.19 us  [shards(): from_low = lax.ppermute(low, 'row', forward)]
    ppermute x0 -> x15, starting transfers between devices: none -> 31.4 us  [shards(): lines.append(lax.ppermute(messages[k], 'col', pairs))]
    ppermute x0 -> x15, waiting for transfers between devices: none -> 23.8 us  [shards(): lines.append(lax.ppermute(messages[k], 'col', pairs))]
    unnamed x23 -> x40, local copies, waits for them, and re-layouts: 17.1 us -> 5.13 us
    all_to_all x1 -> x0, starting transfers between devices: 8.56 us -> none  [shards(): lax.all_to_all(inner, 'col', split_axis=0, concat_axis=0, tiled=True)]
    pallas_call x4 -> x5, Pallas kernels: 29.3 us -> 33.9 us  [the longest x2 25.6 us: finish(): pl.pallas_call(body, grid=(zfull // NBLK,), in_specs=[hbm] * nin + [pl.Bl...]
    all_to_all x1, waiting for transfers between devices: 2.02 us -> 0.01 us  [shards(): lax.all_to_all(edge, 'col', split_axis=0, concat_axis=0, tiled=True)]
    ppermute x1, starting transfers between devices: 0.31 us -> 2.03 us  [shards(): from_low = lax.ppermute(low, 'row', forward)]
  transfers between devices with their start and end apart: 4 -> 18, of which waited for: 2 -> 7; matrix products, arithmetic and copies ran while one was open for 0% -> 0% of each run, Pallas kernels for 15% -> 13%
where the time goes in v2:
time: 114 us
  starting transfers between devices  46.7 us (41%)
  Pallas kernels  33.9 us (30%)
  waiting for transfers between devices  27 us (24%)
  local copies, waits for them, and re-layouts  5.13 us (4%)
    ppermute x15, starting transfers between devices, shards(): lines.append(lax.ppermute(messages[k], 'col', pairs))  31.4 us
    pallas_call x2, Pallas kernels, finish(): pl.pallas_call(body, grid=(zfull // NBLK,), in_specs=[hbm] * nin + [pl.Bl...  25.6 us
    ppermute x15, waiting for transfers between devices, shards(): lines.append(lax.ppermute(messages[k], 'col', pairs))  23.8 us
    all_to_all x1, starting transfers between devices, shards(): lax.all_to_all(edge, 'col', split_axis=0, concat_axis=0, tiled=True)  7.9 us
    ppermute x1, starting transfers between devices, shards(): from_high = lax.ppermute(high, 'row', backward)  5.3 us
    unnamed x40, local copies, waits for them, and re-layouts  5.13 us
    pallas_call x1, Pallas kernels, edge_filter(): pl.pallas_call(edge_body, grid=(xcount // size,), in_specs=[pl.BlockSpec(...  3.69 us
    pallas_call x1, Pallas kernels, inner_filter(): pl.pallas_call(rest_body, in_specs=[hbm, vmem, vmem], out_specs=[vmem] *...  3.21 us
  transfers between devices with their start and end apart: 18, of which 7 were waited for; matrix products, arithmetic and copies ran while one was open for 0% of the time, Pallas kernels for 13%

profile of v2, /device:TPU:1, one launch (start us, length us, event | category | flops | bytes accessed | tf_op | source)
XLA Modules:
  0.0 113.7 jit_solution(7173306805845661124)
XLA Ops:
  0.6 2.2 %copy-done = bf16[128,128,128]{2,1,0:T(8,128)(2,1)S(1)} copy-done((bf16[128,128,128]{2,1,0:T(8,128)(2,1)S(1)}, bf16[128,128,128]{2,1,0:T(8,128)(2,1)}, u32[]{:S(2)}) %copy-start) | copy-done | bytes 4194328
  2.8 0.7 copy-done.2
  3.6 0.8 copy-done.3
  4.4 1.4 %first_messages.1 = (bf16[8,96,128]{2,1,0:T(8,128)(2,1)S(1)}, bf16[8,96,128]{2,1,0:T(8,128)(2,1)S(1)}, bf16[8,96,128]{2,1,0:T(8,128)(2,1)S(1)}, bf16[8,96,128]{2,1,0:T(8,128)(2,1)S(1)}, f32[16,128,128]{2,1,0:T(8,128)S(1)}) custom-call(bf16[128,128,128]{2,1,0:T(8,128)(2,1)S(1)} %copy-done, s32[16,8,128]{2,1,0:T(8,128)S(1)} %bitcast.2, ...), custom_call_target="tpu_custom_call" | custom-call | tf_op jit(solution)/shard_map/first_messages/pallas_call | solution.py:143
  5.8 3.2 %rest_messages.1 = (bf16[8,96,128]{2,1,0:T(8,128)(2,1)S(1)}, bf16[8,96,128]{2,1,0:T(8,128)(2,1)S(1)}, bf16[8,96,128]{2,1,0:T(8,128)(2,1)S(1)}, bf16[8,96,128]{2,...) custom-call(bf16[128,128,128]{2,1,0:T(8,128)(2,1)S(1)} %copy-done, ...), custom_call_target="tpu_custom_call" | custom-call | tf_op jit(solution)/shard_map/rest_messages/pallas_call | solution.py:153
  9.1 0.7 copy-done.1
  9.7 2.0 %collective-permute-start = (bf16[128,4,128]{2,1,0:T(4,128)(2,1)S(1)}, bf16[128,4,128]{2,1,0:T(4,128)(2,1)S(1)}, u32[]{:S(2)}, u32[]{:S(2)}) collective-permute-start(bf16[128,4,128]{2,1,0:T(4,128)(2,1)S(1)} %get-tuple-element.24), channel_id=1, source_target_pairs={{0,16},{16,32},{32,48},{48,64},{64,80},{80,96},{96,112},{112,128},... | collective-permute-start | bytes 393224 | tf_op jit(solution)/shard_map/ppermute | solution.py:345
  11.8 5.3 %collective-permute-start.1 = (bf16[128,4,128]{2,1,0:T(4,128)(2,1)S(1)}, bf16[128,4,128]{2,1,0:T(4,128)(2,1)S(1)}, u32[]{:S(2)}, u32[]{:S(2)}) collective-permute-start(bf16[128,4,128]{2,1,0:T(4,128)(2,1)S(1)} %get-tuple-element.25), channel_id=1, source_target_pairs={{16,0},{32,16},{48,32},{64,48},{80,64},{96,80},{112,96},{128,112},... | collective-permute-start | bytes 393224 | tf_op jit(solution)/shard_map/ppermute | solution.py:346
  17.1 3.2 %collective-permute-done.low_ref = bf16[128,4,128]{2,1,0:T(4,128)(2,1)S(1)} collective-permute-done((bf16[128,4,128]{2,1,0:T(4,128)(2,1)S(1)}, bf16[128,4,128]{2,1,0:T(4,128)(2,1)S(1)}, u32[]{:S(2)}, u32[]{:S(2)}) %collective-permute-start) | collective-permute-done | bytes 131104 | tf_op jit(solution)/shard_map/ppermute | solution.py:345
  20.2 0.0 collective-permute-done.1.high_ref
  20.2 0.0 copy-done.4
  20.3 3.7 %edge_filter.1 = bf16[128,32,128]{2,1,0:T(8,128)(2,1)} custom-call(bf16[128,128,128]{2,1,0:T(8,128)(2,1)S(1)} %copy-done, f32[16,128,128]{2,1,0:T(8,128)S(1)} %get-tuple-element.23.keep_ref, bf16[32,80]{1,0:T(8,128)(2,1)S(1)} %copy-done.4, bf16[128,4,128]{2,1,0:T(4,128)(2,1)S(1)} %collective-permute-done.low_ref, ...), custom_call_target="tpu_custom_call" | custom-call | tf_op jit(solution)/shard_map/edge_filter/pallas_call | solution.py:194
  23.9 7.9 %all-to-all-start = ((bf16[128,32,128]{2,1,0:T(8,128)(2,1)}), bf16[128,32,128]{2,1,0:T(8,128)(2,1)}, u32[]{:S(2)}, u32[]{:S(2)}) async-start(bf16[128,32,128]{2,1,0:T(8,128)(2,1)} %edge_filter.1), calls=%async_computation | async-start | bytes 2097152 | tf_op jit(solution)/shard_map/all_to_all | solution.py:348
  31.8 2.9 %collective-permute-start.2 = (bf16[8,96,128]{2,1,0:T(8,128)(2,1)S(1)}, bf16[8,96,128]{2,1,0:T(8,128)(2,1)S(1)}, u32[]{:S(2)}, u32[]{:S(2)}) collective-permute-start(bf16[8,96,128]{2,1,0:T(8,128)(2,1)S(1)} %get-tuple-element.26), channel_id=1, source_target_pairs={{0,8},{1,9},{2,10},{3,11},{4,12},{5,13},{6,14},{7,15},{8,0},{9,1},... | collective-permute-start | bytes 589832 | tf_op jit(solution)/shard_map/ppermute | solution.py:341
  34.7 1.2 %collective-permute-start.3 = (bf16[8,96,128]{2,1,0:T(8,128)(2,1)S(1)}, bf16[8,96,128]{2,1,0:T(8,128)(2,1)S(1)}, u32[]{:S(2)}, u32[]{:S(2)}) collective-permute-start(bf16[8,96,128]{2,1,0:T(8,128)(2,1)S(1)} %get-tuple-element.27), channel_id=1, source_target_pairs={{0,2},{1,3},{2,4},{3,5},{4,6},{5,7},{6,0},{7,1},{8,10},{9,11},{10,... | collective-permute-start | bytes 589832 | tf_op jit(solution)/shard_map/ppermute | solution.py:341
  35.9 1.2 %collective-permute-start.4 = (bf16[8,96,128]{2,1,0:T(8,128)(2,1)S(1)}, bf16[8,96,128]{2,1,0:T(8,128)(2,1)S(1)}, u32[]{:S(2)}, u32[]{:S(2)}) collective-permute-start(bf16[8,96,128]{2,1,0:T(8,128)(2,1)S(1)} %get-tuple-element.28), channel_id=1, source_target_pairs={{0,10},{1,11},{2,12},{3,13},{4,14},{5,15},{6,8},{7,9},{8,2},{9,3},... | collective-permute-start | bytes 589832 | tf_op jit(solution)/shard_map/ppermute | solution.py:341
  37.1 1.5 %collective-permute-start.5 = (bf16[8,96,128]{2,1,0:T(8,128)(2,1)S(1)}, bf16[8,96,128]{2,1,0:T(8,128)(2,1)S(1)}, u32[]{:S(2)}, u32[]{:S(2)}) collective-permute-start(bf16[8,96,128]{2,1,0:T(8,128)(2,1)S(1)} %get-tuple-element.29), channel_id=1, source_target_pairs={{0,6},{1,7},{2,0},{3,1},{4,2},{5,3},{6,4},{7,5},{8,14},{9,15},{10,... | collective-permute-start | bytes 589832 | tf_op jit(solution)/shard_map/ppermute | solution.py:341
  38.6 2.7 %collective-permute-start.6 = (bf16[8,96,128]{2,1,0:T(8,128)(2,1)S(1)}, bf16[8,96,128]{2,1,0:T(8,128)(2,1)S(1)}, u32[]{:S(2)}, u32[]{:S(2)}) collective-permute-start(bf16[8,96,128]{2,1,0:T(8,128)(2,1)S(1)} %get-tuple-element.30), channel_id=1, source_target_pairs={{0,14},{1,15},{2,8},{3,9},{4,10},{5,11},{6,12},{7,13},{8,6},{9,7},... | collective-permute-start | bytes 589832 | tf_op jit(solution)/shard_map/ppermute | solution.py:341
  41.2 9.8 %collective-permute-done.2.refs_0_ = bf16[8,96,128]{2,1,0:T(8,128)(2,1)S(1)} collective-permute-done((bf16[8,96,128]{2,1,0:T(8,128)(2,1)S(1)}, bf16[8,96,128]{2,1,0:T(8,128)(2,1)S(1)}, u32[]{:S(2)}, u32[]{:S(2)}) %collective-permute-start.2) | collective-permute-done | bytes 196640 | tf_op jit(solution)/shard_map/ppermute | solution.py:341
  51.0 2.7 %collective-permute-start.7 = (bf16[8,96,128]{2,1,0:T(8,128)(2,1)S(1)}, bf16[8,96,128]{2,1,0:T(8,128)(2,1)S(1)}, u32[]{:S(2)}, u32[]{:S(2)}) collective-permute-start(bf16[8,96,128]{2,1,0:T(8,128)(2,1)S(1)} %get-tuple-element.31), channel_id=1, source_target_pairs={{0,4},{1,5},{2,6},{3,7},{4,0},{5,1},{6,2},{7,3},{8,12},{9,13},{10,... | collective-permute-start | bytes 589832 | tf_op jit(solution)/shard_map/ppermute | solution.py:341
  53.7 0.0 collective-permute-done.3.refs_1_
  53.7 1.0 collective-permute-start.8
  54.7 2.6 %collective-permute-done.4.refs_2_ = bf16[8,96,128]{2,1,0:T(8,128)(2,1)S(1)} collective-permute-done((bf16[8,96,128]{2,1,0:T(8,128)(2,1)S(1)}, bf16[8,96,128]{2,1,0:T(8,128)(2,1)S(1)}, u32[]{:S(2)}, u32[]{:S(2)}) %collective-permute-start.4) | collective-permute-done | bytes 196640 | tf_op jit(solution)/shard_map/ppermute | solution.py:341
  57.3 0.5 collective-permute-start.9
  57.8 0.0 collective-permute-done.5.refs_3_
  57.8 1.4 %collective-permute-start.10 = (bf16[8,96,128]{2,1,0:T(8,128)(2,1)S(1)}, bf16[8,96,128]{2,1,0:T(8,128)(2,1)S(1)}, u32[]{:S(2)}, u32[]{:S(2)}) collective-permute-start(bf16[8,96,128]{2,1,0:T(8,128)(2,1)S(1)} %get-tuple-element.34), channel_id=1, source_target_pairs={{0,9},{1,8},{2,11},{3,10},{4,13},{5,12},{6,15},{7,14},{8,1},{9,0},... | collective-permute-start | bytes 589832 | tf_op jit(solution)/shard_map/ppermute | solution.py:341
  59.3 1.1 collective-permute-done.6.refs_4_
  60.3 3.9 %collective-permute-start.11 = (bf16[8,96,128]{2,1,0:T(8,128)(2,1)S(1)}, bf16[8,96,128]{2,1,0:T(8,128)(2,1)S(1)}, u32[]{:S(2)}, u32[]{:S(2)}) collective-permute-start(bf16[8,96,128]{2,1,0:T(8,128)(2,1)S(1)} %get-tuple-element.35), channel_id=1, source_target_pairs={{0,7},{1,6},{2,1},{3,0},{4,3},{5,2},{6,5},{7,4},{8,15},{9,14},{10,... | collective-permute-start | bytes 589832 | tf_op jit(solution)/shard_map/ppermute | solution.py:341
  64.2 0.0 collective-permute-done.7.refs_5_
  64.2 6.5 %collective-permute-start.12 = (bf16[8,96,128]{2,1,0:T(8,128)(2,1)S(1)}, bf16[8,96,128]{2,1,0:T(8,128)(2,1)S(1)}, u32[]{:S(2)}, u32[]{:S(2)}) collective-permute-start(bf16[8,96,128]{2,1,0:T(8,128)(2,1)S(1)} %get-tuple-element.36), channel_id=1, source_target_pairs={{0,11},{1,10},{2,13},{3,12},{4,15},{5,14},{6,9},{7,8},{8,3},{9,2},... | collective-permute-start | bytes 589832 | tf_op jit(solution)/shard_map/ppermute | solution.py:341
  70.7 0.0 collective-permute-done.8.refs_6_
  70.7 0.0 collective-permute-start.13
  70.7 0.4 collective-permute-done.9.refs_7_
  71.1 1.2 %collective-permute-start.14 = (bf16[8,96,128]{2,1,0:T(8,128)(2,1)S(1)}, bf16[8,96,128]{2,1,0:T(8,128)(2,1)S(1)}, u32[]{:S(2)}, u32[]{:S(2)}) collective-permute-start(bf16[8,96,128]{2,1,0:T(8,128)(2,1)S(1)} %get-tuple-element.38), channel_id=1, source_target_pairs={{0,15},{1,14},{2,9},{3,8},{4,11},{5,10},{6,13},{7,12},{8,7},{9,6},... | collective-permute-start | bytes 589832 | tf_op jit(solution)/shard_map/ppermute | solution.py:341
  72.3 0.0 collective-permute-done.10.refs_8_
  72.3 4.9 %collective-permute-start.15 = (bf16[8,96,128]{2,1,0:T(8,128)(2,1)S(1)}, bf16[8,96,128]{2,1,0:T(8,128)(2,1)S(1)}, u32[]{:S(2)}, u32[]{:S(2)}) collective-permute-start(bf16[8,96,128]{2,1,0:T(8,128)(2,1)S(1)} %get-tuple-element.39), channel_id=1, source_target_pairs={{0,13},{1,12},{2,15},{3,14},{4,9},{5,8},{6,11},{7,10},{8,5},{9,4},... | collective-permute-start | bytes 589832 | tf_op jit(solution)/shard_map/ppermute | solution.py:341
  77.2 0.0 collective-permute-done.11.refs_9_
  77.2 0.0 collective-permute-start.16
  77.2 0.0 collective-permute-done.12.refs_10_
  77.3 5.3 %collective-permute-done.13.refs_11_ = bf16[8,96,128]{2,1,0:T(8,128)(2,1)S(1)} collective-permute-done((bf16[8,96,128]{2,1,0:T(8,128)(2,1)S(1)}, bf16[8,96,128]{2,1,0:T(8,128)(2,1)S(1)}, u32[]{:S(2)}, u32[]{:S(2)}) %collective-permute-start.13) | collective-permute-done | bytes 196640 | tf_op jit(solution)/shard_map/ppermute | solution.py:341
  82.6 0.0 collective-permute-done.14.refs_12_
  82.6 4.6 %collective-permute-done.15.refs_13_ = bf16[8,96,128]{2,1,0:T(8,128)(2,1)S(1)} collective-permute-done((bf16[8,96,128]{2,1,0:T(8,128)(2,1)S(1)}, bf16[8,96,128]{2,1,0:T(8,128)(2,1)S(1)}, u32[]{:S(2)}, u32[]{:S(2)}) %collective-permute-start.15) | collective-permute-done | bytes 196640 | tf_op jit(solution)/shard_map/ppermute | solution.py:341
  87.2 0.0 collective-permute-done.16.refs_14_
  87.3 0.6 copy-done.18
  87.9 0.1 copy-done.19
  88.0 15.2 %finish_first.1 = (bf16[8,128,2048]{2,1,0:T(8,128)(2,1)}, bf16[8,128,2048]{2,1,0:T(8,128)(2,1)}) custom-call(bf16[8,96,128]{2,1,0:T(8,128)(2,1)} %copy-done.5, bf16[8,96,128]{2,1,0:T(8,128)(2,1)} %copy-done.6, bf16[8,96,128]{2,1,0:T(8,128)(2,1)} %copy-done.7, bf16[8,96,128]{2,1,0:T(8,128)(2,1)} %copy-done.8, bf16[8,96,128]{2,1,0:T(8,128)(2,1)} %copy-done.9, ...), custom_call_target="tpu_custom_call" | custom-call | tf_op jit(solution)/shard_map/finish_first/pallas_call | solution.py:304
  103.2 0.0 all-to-all-done
  103.2 10.4 %finish_rest.1 = (bf16[8,128,2048]{2,1,0:T(8,128)(2,1)}, bf16[8,128,2048]{2,1,0:T(8,128)(2,1)}) custom-call(bf16[16,8,32,128]{3,2,1,0:T(8,128)(2,1)} %bitcast.1.refs_0_, bf16[512,256]{1,0:T(8,128)(2,1)} %constant.8.clone.refs_16_.refs_1_, bf16[2048,2048]{1,0:T(8,128)(2,1)} %refs_2_.1, ...), custom_call_target="tpu_custom_call", output_to_operand_aliasing={{0}: (3, {}), {1}: (4, {})} | custom-call | tf_op jit(solution)/shard_map/finish_rest/pallas_call | solution.py:304
  (33 shorter events, 0.1 us)
Async XLA Ops:
  0.6 2.2 %copy-start = (bf16[128,128,128]{2,1,0:T(8,128)(2,1)S(1)}, bf16[128,128,128]{2,1,0:T(8,128)(2,1)}, u32[]{:S(2)}) copy-start(bf16[128,128,128]{2,1,0:T(8,128)(2,1)} %field_ref.5) | copy-start | bytes 12582916
  2.8 0.7 copy-start.2
  3.6 0.8 copy-start.3
  4.4 15.9 %copy-start.4 = (bf16[32,80]{1,0:T(8,128)(2,1)S(1)}, bf16[32,80]{1,0:T(8,128)(2,1)}, u32[]{:S(2)}) copy-start(bf16[32,80]{1,0:T(8,128)(2,1)} %constant.7.clone.taps_ref) | copy-start | bytes 15364
  9.0 0.7 copy-start.1
  9.7 10.5 %collective-permute-start = (bf16[128,4,128]{2,1,0:T(4,128)(2,1)S(1)}, bf16[128,4,128]{2,1,0:T(4,128)(2,1)S(1)}, u32[]{:S(2)}, u32[]{:S(2)}) collective-permute-start(bf16[128,4,128]{2,1,0:T(4,128)(2,1)S(1)} %get-tuple-element.24), channel_id=1, source_target_pairs={{0,16},{16,32},{32,48},{48,64},{64,80},{80,96},{96,112},{112,128},... | collective-permute-start | bytes 393224 | tf_op jit(solution)/shard_map/ppermute | solution.py:345
  11.8 8.5 %collective-permute-start.1 = (bf16[128,4,128]{2,1,0:T(4,128)(2,1)S(1)}, bf16[128,4,128]{2,1,0:T(4,128)(2,1)S(1)}, u32[]{:S(2)}, u32[]{:S(2)}) collective-permute-start(bf16[128,4,128]{2,1,0:T(4,128)(2,1)S(1)} %get-tuple-element.25), channel_id=1, source_target_pairs={{16,0},{32,16},{48,32},{64,48},{80,64},{96,80},{112,96},{128,112},... | collective-permute-start | bytes 393224 | tf_op jit(solution)/shard_map/ppermute | solution.py:346
  23.9 79.3 %all-to-all-start = ((bf16[128,32,128]{2,1,0:T(8,128)(2,1)}), bf16[128,32,128]{2,1,0:T(8,128)(2,1)}, u32[]{:S(2)}, u32[]{:S(2)}) async-start(bf16[128,32,128]{2,1,0:T(8,128)(2,1)} %edge_filter.1), calls=%async_computation | async-start | bytes 2097152 | tf_op jit(solution)/shard_map/all_to_all | solution.py:348
  31.8 19.2 %collective-permute-start.2 = (bf16[8,96,128]{2,1,0:T(8,128)(2,1)S(1)}, bf16[8,96,128]{2,1,0:T(8,128)(2,1)S(1)}, u32[]{:S(2)}, u32[]{:S(2)}) collective-permute-start(bf16[8,96,128]{2,1,0:T(8,128)(2,1)S(1)} %get-tuple-element.26), channel_id=1, source_target_pairs={{0,8},{1,9},{2,10},{3,11},{4,12},{5,13},{6,14},{7,15},{8,0},{9,1},... | collective-permute-start | bytes 589832 | tf_op jit(solution)/shard_map/ppermute | solution.py:341
  34.7 19.0 %collective-permute-start.3 = (bf16[8,96,128]{2,1,0:T(8,128)(2,1)S(1)}, bf16[8,96,128]{2,1,0:T(8,128)(2,1)S(1)}, u32[]{:S(2)}, u32[]{:S(2)}) collective-permute-start(bf16[8,96,128]{2,1,0:T(8,128)(2,1)S(1)} %get-tuple-element.27), channel_id=1, source_target_pairs={{0,2},{1,3},{2,4},{3,5},{4,6},{5,7},{6,0},{7,1},{8,10},{9,11},{10,... | collective-permute-start | bytes 589832 | tf_op jit(solution)/shard_map/ppermute | solution.py:341
  35.9 21.5 %collective-permute-start.4 = (bf16[8,96,128]{2,1,0:T(8,128)(2,1)S(1)}, bf16[8,96,128]{2,1,0:T(8,128)(2,1)S(1)}, u32[]{:S(2)}, u32[]{:S(2)}) collective-permute-start(bf16[8,96,128]{2,1,0:T(8,128)(2,1)S(1)} %get-tuple-element.28), channel_id=1, source_target_pairs={{0,10},{1,11},{2,12},{3,13},{4,14},{5,15},{6,8},{7,9},{8,2},{9,3},... | collective-permute-start | bytes 589832 | tf_op jit(solution)/shard_map/ppermute | solution.py:341
  37.1 20.8 %collective-permute-start.5 = (bf16[8,96,128]{2,1,0:T(8,128)(2,1)S(1)}, bf16[8,96,128]{2,1,0:T(8,128)(2,1)S(1)}, u32[]{:S(2)}, u32[]{:S(2)}) collective-permute-start(bf16[8,96,128]{2,1,0:T(8,128)(2,1)S(1)} %get-tuple-element.29), channel_id=1, source_target_pairs={{0,6},{1,7},{2,0},{3,1},{4,2},{5,3},{6,4},{7,5},{8,14},{9,15},{10,... | collective-permute-start | bytes 589832 | tf_op jit(solution)/shard_map/ppermute | solution.py:341
  38.6 21.8 %collective-permute-start.6 = (bf16[8,96,128]{2,1,0:T(8,128)(2,1)S(1)}, bf16[8,96,128]{2,1,0:T(8,128)(2,1)S(1)}, u32[]{:S(2)}, u32[]{:S(2)}) collective-permute-start(bf16[8,96,128]{2,1,0:T(8,128)(2,1)S(1)} %get-tuple-element.30), channel_id=1, source_target_pairs={{0,14},{1,15},{2,8},{3,9},{4,10},{5,11},{6,12},{7,13},{8,6},{9,7},... | collective-permute-start | bytes 589832 | tf_op jit(solution)/shard_map/ppermute | solution.py:341
  51.0 36.2 %copy-start.5 = (bf16[8,96,128]{2,1,0:T(8,128)(2,1)}, bf16[8,96,128]{2,1,0:T(8,128)(2,1)S(1)}, u32[]{:S(2)}) copy-start(bf16[8,96,128]{2,1,0:T(8,128)(2,1)S(1)} %collective-permute-done.2.refs_0_) | copy-start | bytes 589828
  51.0 13.2 %collective-permute-start.7 = (bf16[8,96,128]{2,1,0:T(8,128)(2,1)S(1)}, bf16[8,96,128]{2,1,0:T(8,128)(2,1)S(1)}, u32[]{:S(2)}, u32[]{:S(2)}) collective-permute-start(bf16[8,96,128]{2,1,0:T(8,128)(2,1)S(1)} %get-tuple-element.31), channel_id=1, source_target_pairs={{0,4},{1,5},{2,6},{3,7},{4,0},{5,1},{6,2},{7,3},{8,12},{9,13},{10,... | collective-permute-start | bytes 589832 | tf_op jit(solution)/shard_map/ppermute | solution.py:341
  53.7 33.5 %copy-start.6 = (bf16[8,96,128]{2,1,0:T(8,128)(2,1)}, bf16[8,96,128]{2,1,0:T(8,128)(2,1)S(1)}, u32[]{:S(2)}) copy-start(bf16[8,96,128]{2,1,0:T(8,128)(2,1)S(1)} %collective-permute-done.3.refs_1_) | copy-start | bytes 589828
  53.7 17.0 %collective-permute-start.8 = (bf16[8,96,128]{2,1,0:T(8,128)(2,1)S(1)}, bf16[8,96,128]{2,1,0:T(8,128)(2,1)S(1)}, u32[]{:S(2)}, u32[]{:S(2)}) collective-permute-start(bf16[8,96,128]{2,1,0:T(8,128)(2,1)S(1)} %get-tuple-element.32), channel_id=1, source_target_pairs={{0,12},{1,13},{2,14},{3,15},{4,8},{5,9},{6,10},{7,11},{8,4},{9,5},... | collective-permute-start | bytes 589832 | tf_op jit(solution)/shard_map/ppermute | solution.py:341
  57.3 29.9 %copy-start.7 = (bf16[8,96,128]{2,1,0:T(8,128)(2,1)}, bf16[8,96,128]{2,1,0:T(8,128)(2,1)S(1)}, u32[]{:S(2)}) copy-start(bf16[8,96,128]{2,1,0:T(8,128)(2,1)S(1)} %collective-permute-done.4.refs_2_) | copy-start | bytes 589828
  57.3 13.8 %collective-permute-start.9 = (bf16[8,96,128]{2,1,0:T(8,128)(2,1)S(1)}, bf16[8,96,128]{2,1,0:T(8,128)(2,1)S(1)}, u32[]{:S(2)}, u32[]{:S(2)}) collective-permute-start(bf16[8,96,128]{2,1,0:T(8,128)(2,1)S(1)} %get-tuple-element.33), channel_id=1, source_target_pairs={{0,3},{1,2},{2,5},{3,4},{4,7},{5,6},{6,1},{7,0},{8,11},{9,10},{10,... | collective-permute-start | bytes 589832 | tf_op jit(solution)/shard_map/ppermute | solution.py:341
  57.8 29.4 %copy-start.8 = (bf16[8,96,128]{2,1,0:T(8,128)(2,1)}, bf16[8,96,128]{2,1,0:T(8,128)(2,1)S(1)}, u32[]{:S(2)}) copy-start(bf16[8,96,128]{2,1,0:T(8,128)(2,1)S(1)} %collective-permute-done.5.refs_3_) | copy-start | bytes 589828
  57.8 14.4 %collective-permute-start.10 = (bf16[8,96,128]{2,1,0:T(8,128)(2,1)S(1)}, bf16[8,96,128]{2,1,0:T(8,128)(2,1)S(1)}, u32[]{:S(2)}, u32[]{:S(2)}) collective-permute-start(bf16[8,96,128]{2,1,0:T(8,128)(2,1)S(1)} %get-tuple-element.34), channel_id=1, source_target_pairs={{0,9},{1,8},{2,11},{3,10},{4,13},{5,12},{6,15},{7,14},{8,1},{9,0},... | collective-permute-start | bytes 589832 | tf_op jit(solution)/shard_map/ppermute | solution.py:341
  60.3 26.9 %copy-start.9 = (bf16[8,96,128]{2,1,0:T(8,128)(2,1)}, bf16[8,96,128]{2,1,0:T(8,128)(2,1)S(1)}, u32[]{:S(2)}) copy-start(bf16[8,96,128]{2,1,0:T(8,128)(2,1)S(1)} %collective-permute-done.6.refs_4_) | copy-start | bytes 589828
  60.3 16.9 %collective-permute-start.11 = (bf16[8,96,128]{2,1,0:T(8,128)(2,1)S(1)}, bf16[8,96,128]{2,1,0:T(8,128)(2,1)S(1)}, u32[]{:S(2)}, u32[]{:S(2)}) collective-permute-start(bf16[8,96,128]{2,1,0:T(8,128)(2,1)S(1)} %get-tuple-element.35), channel_id=1, source_target_pairs={{0,7},{1,6},{2,1},{3,0},{4,3},{5,2},{6,5},{7,4},{8,15},{9,14},{10,... | collective-permute-start | bytes 589832 | tf_op jit(solution)/shard_map/ppermute | solution.py:341
  64.2 23.0 %copy-start.10 = (bf16[8,96,128]{2,1,0:T(8,128)(2,1)}, bf16[8,96,128]{2,1,0:T(8,128)(2,1)S(1)}, u32[]{:S(2)}) copy-start(bf16[8,96,128]{2,1,0:T(8,128)(2,1)S(1)} %collective-permute-done.7.refs_5_) | copy-start | bytes 589828
  64.2 13.0 %collective-permute-start.12 = (bf16[8,96,128]{2,1,0:T(8,128)(2,1)S(1)}, bf16[8,96,128]{2,1,0:T(8,128)(2,1)S(1)}, u32[]{:S(2)}, u32[]{:S(2)}) collective-permute-start(bf16[8,96,128]{2,1,0:T(8,128)(2,1)S(1)} %get-tuple-element.36), channel_id=1, source_target_pairs={{0,11},{1,10},{2,13},{3,12},{4,15},{5,14},{6,9},{7,8},{8,3},{9,2},... | collective-permute-start | bytes 589832 | tf_op jit(solution)/shard_map/ppermute | solution.py:341
  70.7 16.6 %copy-start.11 = (bf16[8,96,128]{2,1,0:T(8,128)(2,1)}, bf16[8,96,128]{2,1,0:T(8,128)(2,1)S(1)}, u32[]{:S(2)}) copy-start(bf16[8,96,128]{2,1,0:T(8,128)(2,1)S(1)} %collective-permute-done.8.refs_6_) | copy-start | bytes 589828
  70.7 11.9 %collective-permute-start.13 = (bf16[8,96,128]{2,1,0:T(8,128)(2,1)S(1)}, bf16[8,96,128]{2,1,0:T(8,128)(2,1)S(1)}, u32[]{:S(2)}, u32[]{:S(2)}) collective-permute-start(bf16[8,96,128]{2,1,0:T(8,128)(2,1)S(1)} %get-tuple-element.37), channel_id=1, source_target_pairs={{0,5},{1,4},{2,7},{3,6},{4,1},{5,0},{6,3},{7,2},{8,13},{9,12},{10,... | collective-permute-start | bytes 589832 | tf_op jit(solution)/shard_map/ppermute | solution.py:341
  71.1 16.1 %copy-start.12 = (bf16[8,96,128]{2,1,0:T(8,128)(2,1)}, bf16[8,96,128]{2,1,0:T(8,128)(2,1)S(1)}, u32[]{:S(2)}) copy-start(bf16[8,96,128]{2,1,0:T(8,128)(2,1)S(1)} %collective-permute-done.9.refs_7_) | copy-start | bytes 589828
  71.1 11.4 %collective-permute-start.14 = (bf16[8,96,128]{2,1,0:T(8,128)(2,1)S(1)}, bf16[8,96,128]{2,1,0:T(8,128)(2,1)S(1)}, u32[]{:S(2)}, u32[]{:S(2)}) collective-permute-start(bf16[8,96,128]{2,1,0:T(8,128)(2,1)S(1)} %get-tuple-element.38), channel_id=1, source_target_pairs={{0,15},{1,14},{2,9},{3,8},{4,11},{5,10},{6,13},{7,12},{8,7},{9,6},... | collective-permute-start | bytes 589832 | tf_op jit(solution)/shard_map/ppermute | solution.py:341
  72.3 15.0 %copy-start.13 = (bf16[8,96,128]{2,1,0:T(8,128)(2,1)}, bf16[8,96,128]{2,1,0:T(8,128)(2,1)S(1)}, u32[]{:S(2)}) copy-start(bf16[8,96,128]{2,1,0:T(8,128)(2,1)S(1)} %collective-permute-done.10.refs_8_) | copy-start | bytes 589828
  72.3 14.9 %collective-permute-start.15 = (bf16[8,96,128]{2,1,0:T(8,128)(2,1)S(1)}, bf16[8,96,128]{2,1,0:T(8,128)(2,1)S(1)}, u32[]{:S(2)}, u32[]{:S(2)}) collective-permute-start(bf16[8,96,128]{2,1,0:T(8,128)(2,1)S(1)} %get-tuple-element.39), channel_id=1, source_target_pairs={{0,13},{1,12},{2,15},{3,14},{4,9},{5,8},{6,11},{7,10},{8,5},{9,4},... | collective-permute-start | bytes 589832 | tf_op jit(solution)/shard_map/ppermute | solution.py:341
  77.2 10.0 %copy-start.14 = (bf16[8,96,128]{2,1,0:T(8,128)(2,1)}, bf16[8,96,128]{2,1,0:T(8,128)(2,1)S(1)}, u32[]{:S(2)}) copy-start(bf16[8,96,128]{2,1,0:T(8,128)(2,1)S(1)} %collective-permute-done.11.refs_9_) | copy-start | bytes 589828
  77.2 10.0 %collective-permute-start.16 = (bf16[8,96,128]{2,1,0:T(8,128)(2,1)S(1)}, bf16[8,96,128]{2,1,0:T(8,128)(2,1)S(1)}, u32[]{:S(2)}, u32[]{:S(2)}) collective-permute-start(bf16[8,96,128]{2,1,0:T(8,128)(2,1)S(1)} %get-tuple-element.40), channel_id=1, source_target_pairs={{0,1},{1,0},{2,3},{3,2},{4,5},{5,4},{6,7},{7,6},{8,9},{9,8},{10,11... | collective-permute-start | bytes 589832 | tf_op jit(solution)/shard_map/ppermute | solution.py:341
  77.2 10.0 %copy-start.15 = (bf16[8,96,128]{2,1,0:T(8,128)(2,1)}, bf16[8,96,128]{2,1,0:T(8,128)(2,1)S(1)}, u32[]{:S(2)}) copy-start(bf16[8,96,128]{2,1,0:T(8,128)(2,1)S(1)} %collective-permute-done.12.refs_10_) | copy-start | bytes 589828
  82.6 4.7 %copy-start.16 = (bf16[8,96,128]{2,1,0:T(8,128)(2,1)}, bf16[8,96,128]{2,1,0:T(8,128)(2,1)S(1)}, u32[]{:S(2)}) copy-start(bf16[8,96,128]{2,1,0:T(8,128)(2,1)S(1)} %collective-permute-done.13.refs_11_) | copy-start | bytes 589828
  82.6 4.7 %copy-start.17 = (bf16[8,96,128]{2,1,0:T(8,128)(2,1)}, bf16[8,96,128]{2,1,0:T(8,128)(2,1)S(1)}, u32[]{:S(2)}) copy-start(bf16[8,96,128]{2,1,0:T(8,128)(2,1)S(1)} %collective-permute-done.14.refs_12_) | copy-start | bytes 589828
  87.2 0.7 copy-start.18
  87.2 0.8 copy-start.19
